TPU v7x, 16 devices: a whole 2x2x2 slice. The times are simulated.
16 devices in a mesh: dp: 4 (over z, y), sp: 4 (over x, core).
Axes of the slice: x: 2, y: 2, z: 2, core: 2. Of those that a mesh axis runs over, the one named last changes fastest.
Arguments:
- patches: bfloat16 [8, 3072, 1536], P('dp', 'sp'), parts along dimension 0
- vis_mask: int32 [8, 3072], P('dp', 'sp'), parts along dimension 0
- enc_pos: bfloat16 [12288, 768], P(('dp', 'sp')), parts along dimension 0
- dec_pos: bfloat16 [12288, 384], P(('dp', 'sp')), parts along dimension 0
- w_pe: bfloat16 [1536, 768], replicated
- b_pe: bfloat16 [768], replicated
- enc_qkv: bfloat16 [2, 768, 3, 12, 64], replicated
- enc_proj: bfloat16 [2, 12, 64, 768], replicated
- enc_up: bfloat16 [2, 768, 3072], replicated
- enc_down: bfloat16 [2, 3072, 768], replicated
- w_ed: bfloat16 [768, 384], replicated
- mask_token: bfloat16 [384], replicated
- dec_qkv: bfloat16 [2, 384, 3, 6, 64], replicated
- dec_proj: bfloat16 [2, 6, 64, 384], replicated
- dec_up: bfloat16 [2, 384, 1536], replicated
- dec_down: bfloat16 [2, 1536, 384], replicated
- w_out: bfloat16 [384, 1536], replicated
Outputs:
- output: float32 [8, 3072, 1536], P('dp', 'sp'), parts along dimension 0
There are 4 independent parts. A program takes and returns all parts, laid end to end along the dimension named above; an argument that names none is the same for every part.
All inputs are finite; a program needn't handle non-finite values.
Results may differ from a plain program's by a relative error of at most 0.0157076.
Values are sent between devices in bfloat16 or wider.
A program may use at most 1 GiB of HBM per device.

v0:
```python
import functools
import math

import jax
import jax.numpy as jnp
from jax import lax
from jax.experimental import pallas as pl
from jax.experimental.pallas import tpu as pltpu
from jax.sharding import PartitionSpec as P

F32 = jnp.float32
BF16 = jnp.bfloat16
MESH = pl.DeviceIdType.MESH
VMEM = pl.BlockSpec(memory_space=pltpu.VMEM)
ANY = pl.BlockSpec(memory_space=pl.ANY)

SP = 4
CLIPS = 2
TOK = 768
PATCH = 1536
DIM = 768
ENC_HEADS = 12
HEAD = 64
DDIM = 384
DEC_HEADS = 6
VIS = 96
WIN = 2 * VIS
ROWS = SP * VIS
OWN = 2 * TOK
SEQ = SP * TOK
LAYERS = 2
EXP_SCALE = HEAD ** -0.5 * math.log2(math.e)


def dot(lhs, rhs):
    return jnp.dot(lhs, rhs, preferred_element_type=F32)


def dot_nt(lhs, rhs):
    return lax.dot_general(lhs, rhs, (((1,), (1,)), ((), ())), preferred_element_type=F32)


def dot_tn(lhs, rhs):
    return lax.dot_general(lhs, rhs, (((0,), (0,)), ((), ())), preferred_element_type=F32)


def layer_norm(hidden):
    hid = hidden.astype(F32)
    centred = hid - jnp.mean(hid, axis=-1, keepdims=True)
    var = jnp.mean(centred * centred, axis=-1, keepdims=True)
    return (centred * lax.rsqrt(var + 1e-6)).astype(BF16)


def gelu(val):
    return (0.5 * val * (1.0 + lax.erf(val * math.sqrt(0.5)))).astype(BF16)


def col_max(val):
    return jnp.max(val, axis=0, keepdims=True)


def col_sum(val):
    return jnp.sum(val, axis=0, keepdims=True)


MINE = ROWS // 2
Q_PAD = 256


def encoder_kernel(mask_ref, bpe_ref, token_ref, patch_hbm, pos_hbm, wpe_hbm, dec_pos_hbm, wed_ref, qkv_hbm, proj_hbm, up_hbm, down_hbm,
                   z_ref, rank_ref, pos_out,
                   patch, pos, wpe, qkv, proj, up, down, masks, sendbuf, win, hall, hid, norm, norm_q, q_t, k_n, v_t, o_t,
                   in_sem, w_sem, mask_send, mask_recv, win_send, win_recv, pos_send, pos_recv, row_send, row_recv):
    me = lax.axis_index('sp')
    chip = me // 2
    core = me - 2 * chip
    peer = lax.rem(me + 2, SP)
    sib = me + 1 - 2 * core
    diag = lax.rem(sib + 2, SP)

    loads = [pltpu.make_async_copy(src, dst, in_sem.at[idx])
             for idx, (src, dst) in enumerate(((patch_hbm, patch), (wpe_hbm, wpe), (pos_hbm, pos)))]
    for copy in loads:
        copy.start()
    barrier = pltpu.get_barrier_semaphore()
    for other in (peer, sib, diag):
        pl.semaphore_signal(barrier, inc=1, device_id={'sp': other}, device_id_type=MESH)
    order_row = lax.broadcasted_iota(jnp.int32, (TOK, TOK), 0)
    order_col = lax.broadcasted_iota(jnp.int32, (TOK, TOK), 1)
    before = jnp.where(order_row < order_col, 1.0, 0.0).astype(BF16)
    mine = mask_ref[...].astype(F32)
    mine_rank = dot(jnp.concatenate([mine] * SP, axis=0).astype(BF16), before)[0:CLIPS]
    slot_of = jnp.where(mine > 0.0, mine_rank, -1.0)
    pl.semaphore_wait(barrier, 3)

    def send(src, dst, send_sem, recv_sem, dev):
        copy = pltpu.make_async_remote_copy(
            src_ref=src, dst_ref=dst, send_sem=send_sem, recv_sem=recv_sem, device_id={'sp': dev}, device_id_type=MESH)
        copy.start()
        return copy

    mask_copies = [send(mask_ref, masks.at[step - 1], mask_send.at[step - 1], mask_recv.at[step - 1], lax.rem(me + step, SP))
                   for step in range(1, SP)]
    for copy in loads:
        copy.wait()
    copies = []
    for layer in range(LAYERS):
        for idx, (src, dst) in enumerate(((qkv_hbm, qkv), (proj_hbm, proj), (up_hbm, up), (down_hbm, down))):
            copy = pltpu.make_async_copy(src.at[layer], dst.at[layer], w_sem.at[layer * 4 + idx])
            copy.start()
            copies.append(copy)

    def window(clip, slots):
        rows = lax.broadcasted_iota(jnp.int32, (WIN, TOK), 0).astype(F32)
        hit = jnp.where(rows == slots, 1.0, 0.0)
        select = hit.astype(BF16)
        moved = dot(select, patch[clip]).astype(BF16)
        occupied = jnp.sum(hit, axis=1, keepdims=True)
        emb = dot(moved, wpe[...]) + occupied * bpe_ref[...].astype(F32) + dot(select, pos[...])
        return emb.astype(BF16)

    far = jnp.where(chip == 0, slot_of[1:2], slot_of[0:1])
    near = jnp.where(chip == 0, slot_of[0:1], slot_of[1:2])
    sendbuf[...] = window(1 - chip, far)
    to_peer = send(sendbuf, win.at[1], win_send.at[0], win_recv.at[0], peer)
    win[0] = window(chip, near)
    to_sib = send(win.at[0], win.at[2], win_send.at[1], win_recv.at[1], sib)

    for copy in mask_copies:
        copy.wait()
    stacked = jnp.concatenate([mine] + [masks[k].astype(F32) for k in range(SP - 1)], axis=0)
    local = dot(stacked.astype(BF16), before)
    counts = jnp.sum(stacked, axis=1, keepdims=True)
    row_dev = lax.rem(me - lax.broadcasted_iota(jnp.int32, (CLIPS * SP, 1), 0) // CLIPS + SP, SP)
    base = jnp.zeros((CLIPS * SP, 1), F32)
    for k in range(SP):
        dev_k = lax.rem(me - k + SP, SP)
        tiled = jnp.concatenate([counts[CLIPS * k:CLIPS * k + CLIPS]] * SP, axis=0)
        base = base + jnp.where(dev_k < row_dev, tiled, 0.0)
    rank_ref[...] = jnp.where(stacked > 0.0, local + base, float(ROWS)).astype(jnp.int32)

    def placement(slot):
        def pick(val):
            two = val[CLIPS * slot:CLIPS * slot + CLIPS]
            return jnp.where(chip == 0, two[0:1], two[1:2])

        start, size = pick(base), pick(counts)
        rows = lax.broadcasted_iota(jnp.int32, (ROWS, WIN), 0).astype(F32)
        cols = lax.broadcasted_iota(jnp.int32, (ROWS, WIN), 1).astype(F32)
        return jnp.where((rows == cols + start) & (cols < size), 1.0, 0.0)

    even = core == 0
    left, right = placement(1), placement(3)
    place = [placement(0), placement(2), jnp.where(even, right, left), jnp.where(even, left, right)]
    to_peer.wait_recv()
    relay = send(win.at[1], win.at[3], win_send.at[2], win_recv.at[2], sib)
    pos_peer = send(dec_pos_hbm, pos_out.at[0], pos_send.at[0], pos_recv.at[0], peer)
    pos_sib = send(dec_pos_hbm, pos_out.at[1], pos_send.at[1], pos_recv.at[1], sib)
    total = dot(place[0].astype(BF16), win[0]) + dot(place[1].astype(BF16), win[1])
    to_sib.wait_recv()
    total = total + dot(place[2].astype(BF16), win[2])
    relay.wait_recv()
    total = total + dot(place[3].astype(BF16), win[3])
    hall[...] = total.astype(BF16)
    own = pl.ds(pl.multiple_of(core * MINE, MINE), MINE)
    hid[...] = hall[own, :]
    norm[0] = layer_norm(hall[...])
    norm_q[MINE:] = jnp.zeros((Q_PAD - MINE, DIM), BF16)
    zero = jnp.zeros((HEAD, Q_PAD), BF16)
    pos_diag = swap = None

    for layer in range(LAYERS):
        copies[layer * 4].wait()
        norm_q[0:MINE] = norm[layer, own, :]
        q_t[...] = dot_nt(qkv[layer, 0:DIM], norm_q[...]).astype(BF16)
        if swap is not None:
            swap.wait()
        k_n[...] = dot_nt(norm[layer], qkv[layer, DIM:2 * DIM]).astype(BF16)
        v_t[...] = dot_nt(qkv[layer, 2 * DIM:3 * DIM], norm[layer]).astype(BF16)

        def heads(group, carry):
            scores, weights = [], []
            for pair in range(2):
                lanes = pl.ds(pl.multiple_of((2 * group + pair) * 2 * HEAD, 2 * HEAD), 2 * HEAD)
                for odd in range(2):
                    rows = pl.ds(pl.multiple_of((4 * group + 2 * pair + odd) * HEAD, HEAD), HEAD)
                    q_head = q_t[rows, :]
                    q_both = jnp.concatenate([zero, q_head] if odd else [q_head, zero], axis=0)
                    scores.append(dot(k_n[:, lanes], q_both))
            for s in scores:
                e = jnp.exp2(s * EXP_SCALE - col_max(s) * EXP_SCALE)
                weights.append((e.astype(BF16), 1.0 / col_sum(e)))
            for idx, (e, scale) in enumerate(weights):
                rows = pl.ds(pl.multiple_of((4 * group + idx) * HEAD, HEAD), HEAD)
                o_t[rows, :] = (dot(v_t[rows, :], e) * scale).astype(BF16)
            return carry

        lax.fori_loop(0, ENC_HEADS // 4, heads, 0)
        if layer == 0:
            pos_peer.wait_recv()
            pos_diag = send(pos_out.at[0], pos_out.at[2], pos_send.at[2], pos_recv.at[2], sib)
        copies[layer * 4 + 1].wait()
        mid = (hid[...].astype(F32) + dot_tn(o_t[...], proj[layer])[0:MINE]).astype(BF16)
        rows_norm = layer_norm(mid)
        copies[layer * 4 + 2].wait()
        copies[layer * 4 + 3].wait()
        acc = None
        for lo in range(0, 4 * DIM, DIM):
            act = gelu(dot(rows_norm, up[layer, :, lo:lo + DIM]))
            part = dot(act, down[layer, lo:lo + DIM, :])
            acc = part if acc is None else acc + part
        out = (mid.astype(F32) + acc).astype(BF16)
        if layer < LAYERS - 1:
            hid[...] = out
            norm[layer + 1, own, :] = layer_norm(out)
            swap = send(norm.at[layer + 1, own], norm.at[layer + 1, own], row_send.at[layer], row_recv.at[layer], sib)
    z_ref[own, :] = dot(layer_norm(out), wed_ref[...]).astype(BF16)
    first = lax.broadcasted_iota(jnp.int32, (2 * HEAD, DDIM), 0) == 0
    z_ref[ROWS:] = jnp.where(first, token_ref[...].astype(F32), 0.0).astype(BF16)
    last = send(z_ref.at[own], z_ref.at[own], row_send.at[LAYERS - 1], row_recv.at[LAYERS - 1], sib)
    to_peer.wait_send()
    to_sib.wait_send()
    relay.wait_send()
    pos_peer.wait_send()
    pos_sib.wait()
    pos_diag.wait()
    last.wait()


def encode(mask, bpe, token, patches, enc_pos, wpe, dec_pos, wed, qkv_t, proj, up, down):
    return pl.pallas_call(
        encoder_kernel,
        out_shape=(
            jax.ShapeDtypeStruct((ROWS + 2 * HEAD, DDIM), BF16),
            jax.ShapeDtypeStruct((CLIPS * SP, TOK), jnp.int32),
            jax.ShapeDtypeStruct((SP - 1, TOK, DDIM), BF16),
        ),
        in_specs=[VMEM] * 3 + [ANY] * 4 + [VMEM] + [ANY] * 4,
        out_specs=(VMEM, VMEM, ANY),
        scratch_shapes=[
            pltpu.VMEM((CLIPS, TOK, PATCH), BF16),
            pltpu.VMEM((TOK, DIM), BF16),
            pltpu.VMEM((PATCH, DIM), BF16),
            pltpu.VMEM((LAYERS, 3 * DIM, DIM), BF16),
            pltpu.VMEM((LAYERS, DIM, DIM), BF16),
            pltpu.VMEM((LAYERS, DIM, 4 * DIM), BF16),
            pltpu.VMEM((LAYERS, 4 * DIM, DIM), BF16),
            pltpu.VMEM((SP - 1, CLIPS, TOK), jnp.int32),
            pltpu.VMEM((WIN, DIM), BF16),
            pltpu.VMEM((SP, WIN, DIM), BF16),
            pltpu.VMEM((ROWS, DIM), BF16),
            pltpu.VMEM((MINE, DIM), BF16),
            pltpu.VMEM((LAYERS, ROWS, DIM), BF16),
            pltpu.VMEM((Q_PAD, DIM), BF16),
            pltpu.VMEM((DIM, Q_PAD), BF16),
            pltpu.VMEM((ROWS, DIM), BF16),
            pltpu.VMEM((DIM, ROWS), BF16),
            pltpu.VMEM((DIM, Q_PAD), BF16),
            pltpu.SemaphoreType.DMA((3,)),
            pltpu.SemaphoreType.DMA((LAYERS * 4,)),
            pltpu.SemaphoreType.DMA((SP - 1,)),
            pltpu.SemaphoreType.DMA((SP - 1,)),
            pltpu.SemaphoreType.DMA((3,)),
            pltpu.SemaphoreType.DMA((3,)),
            pltpu.SemaphoreType.DMA((3,)),
            pltpu.SemaphoreType.DMA((3,)),
            pltpu.SemaphoreType.DMA((LAYERS,)),
            pltpu.SemaphoreType.DMA((LAYERS,)),
        ],
        compiler_params=pltpu.CompilerParams(collective_id=0, has_side_effects=True, vmem_limit_bytes=58 * 2 ** 20),
        cost_estimate=pl.CostEstimate(flops=12 * 10 ** 9, bytes_accessed=4 * 10 ** 7, transcendentals=0),
        name='encoder',
    )(mask, bpe, token, patches, enc_pos, wpe, dec_pos, wed, qkv_t, proj, up, down)


Q_BLK = 512
K_BLK = 256
CHUNK = 256
WIDE = 512
PAIR = 2 * HEAD


def fill_rows(start, count, step, body):
    def run(i, carry):
        body(pl.ds(pl.multiple_of(start + i * step, step), step))
        return carry

    lax.fori_loop(0, count // step, run, 0)


def make_queries(rows, norm, w_q, q_3):
    q = dot_nt(w_q, norm[rows, :]).astype(BF16).astype(F32) * EXP_SCALE
    hi = q.astype(BF16)
    rest = q - hi.astype(F32)
    mid = rest.astype(BF16)
    low = (rest - mid.astype(F32)).astype(BF16)
    zero = jnp.zeros((HEAD, q.shape[1]), BF16)
    for head in range(DEC_HEADS):
        part = slice(head * HEAD, (head + 1) * HEAD)
        tail = (low[part], zero) if head % 2 == 0 else (zero, low[part])
        for idx, val in enumerate((hi[part], mid[part]) + tail):
            q_3[head, idx * HEAD:(idx + 1) * HEAD, rows] = val


def make_keys(rows, norm, w_k, w_v, k_n, k_dup, v_t):
    a = norm[rows, :]
    k = dot_nt(a, w_k)
    k_n[rows, :] = k.astype(BF16)
    first = lax.broadcasted_iota(jnp.int32, (k.shape[0], PAIR), 1) < HEAD
    for pair in range(DEC_HEADS // 2):
        both = k[:, pair * PAIR:(pair + 1) * PAIR]
        turned = pltpu.roll(both, HEAD, axis=1)
        k_dup[rows, 2 * pair * PAIR:(2 * pair + 1) * PAIR] = jnp.where(first, both, turned).astype(BF16)
        k_dup[rows, (2 * pair + 1) * PAIR:(2 * pair + 2) * PAIR] = jnp.where(first, turned, both).astype(BF16)
    v_t[:, rows] = dot_nt(w_v, a).astype(BF16)


def attention(start, count, q_3, k_n, k_dup, v_t, o_t, s_even, s_odd):
    blocks = count // Q_BLK
    units = DEC_HEADS * blocks

    def place(unit):
        head = unit // blocks
        return head, pl.ds(pl.multiple_of(start + (unit - head * blocks) * Q_BLK, Q_BLK), Q_BLK)

    def mixed(unit_q, s_q, unit_p, s_p, max8):
        if unit_q is not None:
            head_q, cols_q = place(unit_q)
            q = q_3[head_q, :, cols_q]
            lanes = pl.ds(pl.multiple_of((head_q // 2) * PAIR, PAIR), PAIR)
            lanes_dup = pl.ds(pl.multiple_of(head_q * PAIR, PAIR), PAIR)
        if unit_p is not None:
            head_p, cols_p = place(unit_p)
            shift = col_max(max8)
            v_rows = pl.ds(pl.multiple_of(head_p * HEAD, HEAD), HEAD)
        new_max = total = late = None
        accs = [None, None]

        def weigh(idx, weights):
            o = dot(v_t[v_rows, idx * K_BLK:(idx + 1) * K_BLK], weights)
            accs[idx % 2] = o if accs[idx % 2] is None else accs[idx % 2] + o

        for idx in range(SEQ // K_BLK):
            rows = slice(idx * K_BLK, (idx + 1) * K_BLK)
            if unit_p is not None:
                e = jnp.exp2(s_p[rows, :] - shift)
                t = jnp.sum(e.reshape(K_BLK // 8, 8, Q_BLK), axis=0)
                total = t if total is None else total + t
                if late is not None:
                    weigh(*late)
                late = (idx, e.astype(BF16))
            if unit_q is not None:
                keys = jnp.concatenate([k_dup[rows, lanes_dup], k_n[rows, lanes]], axis=1)
                s = dot(keys, q)
                s_q[rows, :] = s
                m = jnp.max(s.reshape(K_BLK // 8, 8, Q_BLK), axis=0)
                new_max = m if new_max is None else jnp.maximum(new_max, m)
        if unit_p is not None:
            weigh(*late)
            o_t[v_rows, cols_p] = ((accs[0] + accs[1]) * (1.0 / col_sum(total))).astype(BF16)
        return new_max

    first = mixed(0, s_even, None, None, None)

    def body(i, max8):
        unit = 2 * i
        max_odd = mixed(unit + 1, s_odd, unit, s_even, max8)
        return mixed(jnp.minimum(unit + 2, units - 1), s_even, unit + 1, s_odd, max_odd)

    lax.fori_loop(0, units // 2, body, first)


def mlp(rows, hid, o_t, w_proj, w_up, w_down):
    mid = (hid[rows, :].astype(F32) + dot_tn(o_t[:, rows], w_proj)).astype(BF16)
    act = gelu(dot(layer_norm(mid), w_up))
    return (mid.astype(F32) + dot(act, w_down)).astype(BF16)


def decoder_kernel(z_ref, rank_ref, pos_me, pos_x, qkv_hbm, proj_hbm, up_hbm, down_hbm, both_ref,
                   qkv, proj, up, down, hid, norm, fin, q_3, k_n, k_dup, v_t, o_t, s_even, s_odd, w_sem, ready, row_send, row_recv, fin_send, fin_recv):
    me = lax.axis_index('sp')
    chip = me // 2
    core = me - 2 * chip
    peer = lax.rem(me + 2, SP)
    sib = me + 1 - 2 * core
    diag = lax.rem(sib + 2, SP)

    copies = []
    for layer in range(LAYERS):
        for idx, (src, dst) in enumerate(((qkv_hbm, qkv), (proj_hbm, proj), (up_hbm, up), (down_hbm, down))):
            copy = pltpu.make_async_copy(src.at[layer], dst.at[layer], w_sem.at[layer * 4 + idx])
            copy.start()
            copies.append(copy)
    barrier = pltpu.get_barrier_semaphore()
    for other in (peer, sib):
        pl.semaphore_signal(barrier, inc=1, device_id={'sp': other}, device_id_type=MESH)
    pl.semaphore_wait(barrier, 2)

    def tokens(dev, pos):
        slot = lax.rem(me - dev + SP, SP)
        rank = rank_ref[pl.ds(2 * slot + chip, 1), :]
        rank_col = jnp.transpose(jnp.broadcast_to(rank.astype(F32), (8, TOK)))[:, 0:1]
        lanes = lax.broadcasted_iota(jnp.int32, (TOK, ROWS + 2 * HEAD), 1).astype(F32)
        select = jnp.where(lanes == rank_col, 1.0, 0.0).astype(BF16)
        return (dot(select, z_ref[...]) + pos.astype(F32)).astype(BF16)

    hid[0:TOK] = tokens(peer, pos_x[0])
    hid[TOK:OWN] = tokens(me, pos_me[...])
    norm[OWN:OWN + TOK] = layer_norm(tokens(diag, pos_x[2]))
    norm[OWN + TOK:SEQ] = layer_norm(tokens(sib, pos_x[1]))

    def own_norm(rows):
        norm[rows, :] = layer_norm(hid[rows, :])

    fill_rows(0, OWN, CHUNK, own_norm)

    def queries(layer):
        fill_rows(0, OWN, WIDE, lambda rows: make_queries(rows, norm, qkv[layer, 0:DDIM], q_3))

    def keys(layer, start, count):
        fill_rows(start, count, WIDE, lambda rows: make_keys(
            rows, norm, qkv[layer, DDIM:2 * DDIM], qkv[layer, 2 * DDIM:3 * DDIM], k_n, k_dup, v_t))

    for copy in copies:
        copy.wait()
    queries(0)
    keys(0, 0, SEQ)
    pl.semaphore_signal(ready, inc=1, device_id={'sp': sib}, device_id_type=MESH)
    attention(0, OWN, q_3, k_n, k_dup, v_t, o_t, s_even, s_odd)
    pl.semaphore_wait(ready, 1)
    steps = OWN // CHUNK

    def row_copy(i):
        src = pl.ds(pl.multiple_of(i * CHUNK, CHUNK), CHUNK)
        dst = pl.ds(pl.multiple_of(OWN + i * CHUNK, CHUNK), CHUNK)
        return pltpu.make_async_remote_copy(
            src_ref=norm.at[src], dst_ref=norm.at[dst], send_sem=row_send.at[i], recv_sem=row_recv.at[i],
            device_id={'sp': sib}, device_id_type=MESH)

    def first_mlp(i, carry):
        rows = pl.ds(pl.multiple_of(i * CHUNK, CHUNK), CHUNK)
        val = mlp(rows, hid, o_t, proj[0], up[0], down[0])
        hid[rows, :] = val
        norm[rows, :] = layer_norm(val)

        @pl.when(i > 0)
        def _():
            row_copy(i - 1).start()

        return carry

    lax.fori_loop(0, steps, first_mlp, 0)
    queries(1)
    row_copy(steps - 1).start()
    keys(1, 0, OWN)
    for i in range(steps):
        row_copy(i).wait()
    keys(1, OWN, OWN)

    early = 2 * Q_BLK
    attention(0, early, q_3, k_n, k_dup, v_t, o_t, s_even, s_odd)

    def last_rows(rows):
        fin[rows, :] = layer_norm(mlp(rows, hid, o_t, proj[1], up[1], down[1]))

    fill_rows(0, early, CHUNK, last_rows)
    send = pltpu.make_async_remote_copy(
        src_ref=fin.at[pl.ds(0, TOK)], dst_ref=both_ref.at[chip], send_sem=fin_send, recv_sem=fin_recv,
        device_id={'sp': peer}, device_id_type=MESH)
    send.start()
    attention(early, OWN - early, q_3, k_n, k_dup, v_t, o_t, s_even, s_odd)
    fill_rows(early, OWN - early, CHUNK, last_rows)
    both_ref[chip] = fin[TOK:OWN]
    send.wait()


def decode(z, rank, pos, pos_x, wqkv, wproj, wup, wdown):
    return pl.pallas_call(
        decoder_kernel,
        out_shape=jax.ShapeDtypeStruct((CLIPS, TOK, DDIM), BF16),
        in_specs=[VMEM] * 4 + [ANY] * 4,
        out_specs=VMEM,
        scratch_shapes=[
            pltpu.VMEM((LAYERS, 3 * DDIM, DDIM), BF16),
            pltpu.VMEM((LAYERS, DDIM, DDIM), BF16),
            pltpu.VMEM((LAYERS, DDIM, 4 * DDIM), BF16),
            pltpu.VMEM((LAYERS, 4 * DDIM, DDIM), BF16),
            pltpu.VMEM((OWN, DDIM), BF16),
            pltpu.VMEM((SEQ, DDIM), BF16),
            pltpu.VMEM((OWN, DDIM), BF16),
            pltpu.VMEM((DEC_HEADS, 4 * HEAD, OWN), BF16),
            pltpu.VMEM((SEQ, DDIM), BF16),
            pltpu.VMEM((SEQ, 2 * DDIM), BF16),
            pltpu.VMEM((DDIM, SEQ), BF16),
            pltpu.VMEM((DDIM, OWN), BF16),
            pltpu.VMEM((SEQ, Q_BLK), F32),
            pltpu.VMEM((SEQ, Q_BLK), F32),
            pltpu.SemaphoreType.DMA((LAYERS * 4,)),
            pltpu.SemaphoreType.REGULAR,
            pltpu.SemaphoreType.DMA((OWN // CHUNK,)),
            pltpu.SemaphoreType.DMA((OWN // CHUNK,)),
            pltpu.SemaphoreType.DMA,
            pltpu.SemaphoreType.DMA,
        ],
        compiler_params=pltpu.CompilerParams(collective_id=1, has_side_effects=True, vmem_limit_bytes=58 * 2 ** 20),
        cost_estimate=pl.CostEstimate(flops=60 * 10 ** 9, bytes_accessed=2 * 10 ** 7, transcendentals=6 * 10 ** 7),
        name='decoder',
    )(z, rank, pos, pos_x, wqkv, wproj, wup, wdown)


def solution(mesh):
    def local_program(patches, vis_mask, enc_pos, dec_pos, w_pe, b_pe, enc_qkv, enc_proj, enc_up, enc_down, w_ed, mask_token, dec_qkv, dec_proj, dec_up, dec_down, w_out):
        enc_qkv_t = jnp.transpose(enc_qkv, (0, 2, 3, 4, 1)).reshape(LAYERS, 3 * DIM, DIM)
        dec_qkv_t = jnp.transpose(dec_qkv, (0, 2, 3, 4, 1)).reshape(LAYERS, 3 * DDIM, DDIM)
        enc_proj2 = enc_proj.reshape(LAYERS, DIM, DIM)
        dec_proj2 = dec_proj.reshape(LAYERS, DDIM, DDIM)
        z, rank, pos_x = encode(vis_mask, b_pe.reshape(1, DIM), mask_token.reshape(1, DDIM), patches, enc_pos, w_pe, dec_pos, w_ed,
                                enc_qkv_t, enc_proj2, enc_up, enc_down)
        both = decode(z, rank, dec_pos, pos_x, dec_qkv_t, dec_proj2, dec_up, dec_down)
        return jnp.einsum('cne,ep->cnp', both, w_out, preferred_element_type=F32)

    row_spec = P('dp', 'sp', None)
    pos_spec = P(('dp', 'sp'), None)
    arg_specs = (row_spec, P('dp', 'sp'), pos_spec, pos_spec) + (P(),) * 13
    return jax.shard_map(local_program, mesh=mesh, in_specs=arg_specs, out_specs=row_spec, check_vma=False)
```

profile of v0, /device:TPU:0, one launch (start us, length us, event | category | flops | bytes accessed | tf_op | source)
XLA Modules:
  0.0 154.6 jit_solution(10176514028003936953)
XLA Ops:
  0.0 0.0 copy-start
  0.0 1.4 reshape.19.token_ref
  1.4 1.3 reshape.18.bpe_ref
  2.6 43.6 %encoder.1 = (bf16[512,384]{1,0:T(8,128)(2,1)}, s32[8,768]{1,0:T(8,128)}, bf16[3,768,384]{2,1,0:T(8,128)(2,1)}) custom-call(s32[2,768]{1,0:T(2,128)} %mask_ref.1, bf16[1,768]{1,0:T(2,128)(2,1)} %reshape.18.bpe_ref, bf16[1,384]{1,0:T(2,128)(2,1)} %reshape.19.token_ref, bf16[2,768,1536]{2,1,0:T(8,128)(2,1)} %patch_hbm.1, bf16[768,768]{1,0:T(8,128)(2,1)} %pos_hbm.1, ...), custom_call_target="tpu_custom_call" | custom-call | flops 12000000000 | bytes 40000000 | tf_op jit(solution)/shard_map/encoder/pallas_call | solution.py:231
  46.3 101.9 %decoder.1 = bf16[2,768,384]{2,1,0:T(8,128)(2,1)} custom-call(bf16[512,384]{1,0:T(8,128)(2,1)} %get-tuple-element.8.z_ref, s32[8,768]{1,0:T(8,128)} %get-tuple-element.9.rank_ref, bf16[768,384]{1,0:T(8,128)(2,1)} %pos_me.1, bf16[3,768,384]{2,1,0:T(8,128)(2,1)} %get-tuple-element.10.pos_x, bf16[2,1152,384]{2,1,0:T(8,128)(2,1)} %bitcast.14, ...), custom_call_target="tpu_custom_call" | custom-call | flops 60000002048 | bytes 20000000 | tf_op jit(solution)/shard_map/decoder/pallas_call | solution.py:478
  148.2 0.0 copy-done
  148.2 6.4 %fusion = f32[2,768,1536]{2,1,0:T(8,128)} fusion(bf16[2,768,384]{2,1,0:T(8,128)(2,1)} %decoder.1, bf16[384,1536]{1,0:T(8,128)(2,1)S(1)} %copy-done), kind=kOutput, calls=%fused_computation | convolution fusion | flops 1811939328 | bytes 11796480 | tf_op jit(solution)/shard_map/cne,ep->cnp/dot_general | solution.py:520
Async XLA Ops:
  0.0 148.2 %copy-start = (bf16[384,1536]{1,0:T(8,128)(2,1)S(1)}, bf16[384,1536]{1,0:T(8,128)(2,1)}, u32[]{:S(2)}) copy-start(bf16[384,1536]{1,0:T(8,128)(2,1)} %param.33) | copy-start | bytes 3538948
where the time goes:
time: 155 us
  Pallas kernels  146 us (94%)
  matrix products  6.42 us (4%)
  local copies, waits for them, and re-layouts  2.64 us (2%)
    pallas_call x1, Pallas kernels, decode(): pl.pallas_call(decoder_kernel, out_shape=jax.ShapeDtypeStruct((CLIPS, TOK...  102 us
    pallas_call x1, Pallas kernels, encode(): pl.pallas_call(encoder_kernel, out_shape=(jax.ShapeDtypeStruct((ROWS + 2...  43.6 us
    dot_general x1, matrix products, local_program(): return jnp.einsum('cne,ep->cnp', both, w_out, preferred_element_type=F32)  6.42 us

commit v1 on v0

--- a/solution.py
+++ b/solution.py
@@ -110,13 +110,15 @@
             copy.start()
             copies.append(copy)
 
+    bias = bpe_ref[...].astype(F32).reshape(1, DIM)
+
     def window(clip, slots):
         rows = lax.broadcasted_iota(jnp.int32, (WIN, TOK), 0).astype(F32)
         hit = jnp.where(rows == slots, 1.0, 0.0)
         select = hit.astype(BF16)
         moved = dot(select, patch[clip]).astype(BF16)
         occupied = jnp.sum(hit, axis=1, keepdims=True)
-        emb = dot(moved, wpe[...]) + occupied * bpe_ref[...].astype(F32) + dot(select, pos[...])
+        emb = dot(moved, wpe[...]) + occupied * bias + dot(select, pos[...])
         return emb.astype(BF16)
 
     far = jnp.where(chip == 0, slot_of[1:2], slot_of[0:1])
@@ -196,14 +198,14 @@
             return carry
 
         lax.fori_loop(0, ENC_HEADS // 4, heads, 0)
-        if layer == 0:
-            pos_peer.wait_recv()
-            pos_diag = send(pos_out.at[0], pos_out.at[2], pos_send.at[2], pos_recv.at[2], sib)
         copies[layer * 4 + 1].wait()
         mid = (hid[...].astype(F32) + dot_tn(o_t[...], proj[layer])[0:MINE]).astype(BF16)
         rows_norm = layer_norm(mid)
         copies[layer * 4 + 2].wait()
         copies[layer * 4 + 3].wait()
+        if layer == LAYERS - 1:
+            pos_peer.wait_recv()
+            pos_diag = send(pos_out.at[0], pos_out.at[2], pos_send.at[2], pos_recv.at[2], sib)
         acc = None
         for lo in range(0, 4 * DIM, DIM):
             act = gelu(dot(rows_norm, up[layer, :, lo:lo + DIM]))
@@ -216,7 +218,7 @@
             swap = send(norm.at[layer + 1, own], norm.at[layer + 1, own], row_send.at[layer], row_recv.at[layer], sib)
     z_ref[own, :] = dot(layer_norm(out), wed_ref[...]).astype(BF16)
     first = lax.broadcasted_iota(jnp.int32, (2 * HEAD, DDIM), 0) == 0
-    z_ref[ROWS:] = jnp.where(first, token_ref[...].astype(F32), 0.0).astype(BF16)
+    z_ref[ROWS:] = jnp.where(first, token_ref[...].astype(F32).reshape(1, DDIM), 0.0).astype(BF16)
     last = send(z_ref.at[own], z_ref.at[own], row_send.at[LAYERS - 1], row_recv.at[LAYERS - 1], sib)
     to_peer.wait_send()
     to_sib.wait_send()
@@ -421,13 +423,14 @@
         fill_rows(start, count, WIDE, lambda rows: make_keys(
             rows, norm, qkv[layer, DDIM:2 * DDIM], qkv[layer, 2 * DDIM:3 * DDIM], k_n, k_dup, v_t))
 
-    for copy in copies:
-        copy.wait()
+    copies[0].wait()
     queries(0)
     keys(0, 0, SEQ)
     pl.semaphore_signal(ready, inc=1, device_id={'sp': sib}, device_id_type=MESH)
     attention(0, OWN, q_3, k_n, k_dup, v_t, o_t, s_even, s_odd)
     pl.semaphore_wait(ready, 1)
+    for copy in copies[1:]:
+        copy.wait()
     steps = OWN // CHUNK
 
     def row_copy(i):
@@ -508,16 +511,37 @@
     )(z, rank, pos, pos_x, wqkv, wproj, wup, wdown)
 
 
+OUT_ROWS = 256
+
+
+def output_kernel(both_ref, w_ref, out_ref):
+    out_ref[...] = dot(both_ref[...], w_ref[...])
+
+
+def project(both, w_out):
+    rows = both.reshape(CLIPS * TOK, DDIM)
+    out = pl.pallas_call(
+        output_kernel,
+        grid=(CLIPS * TOK // OUT_ROWS,),
+        out_shape=jax.ShapeDtypeStruct((CLIPS * TOK, PATCH), F32),
+        in_specs=[pl.BlockSpec((OUT_ROWS, DDIM), lambda i: (i, 0)), pl.BlockSpec((DDIM, PATCH), lambda i: (0, 0))],
+        out_specs=pl.BlockSpec((OUT_ROWS, PATCH), lambda i: (i, 0)),
+        cost_estimate=pl.CostEstimate(flops=2 * 10 ** 9, bytes_accessed=12 * 10 ** 6, transcendentals=0),
+        name='output',
+    )(rows, w_out)
+    return out.reshape(CLIPS, TOK, PATCH)
+
+
 def solution(mesh):
     def local_program(patches, vis_mask, enc_pos, dec_pos, w_pe, b_pe, enc_qkv, enc_proj, enc_up, enc_down, w_ed, mask_token, dec_qkv, dec_proj, dec_up, dec_down, w_out):
         enc_qkv_t = jnp.transpose(enc_qkv, (0, 2, 3, 4, 1)).reshape(LAYERS, 3 * DIM, DIM)
         dec_qkv_t = jnp.transpose(dec_qkv, (0, 2, 3, 4, 1)).reshape(LAYERS, 3 * DDIM, DDIM)
         enc_proj2 = enc_proj.reshape(LAYERS, DIM, DIM)
         dec_proj2 = dec_proj.reshape(LAYERS, DDIM, DDIM)
-        z, rank, pos_x = encode(vis_mask, b_pe.reshape(1, DIM), mask_token.reshape(1, DDIM), patches, enc_pos, w_pe, dec_pos, w_ed,
+        z, rank, pos_x = encode(vis_mask, b_pe, mask_token, patches, enc_pos, w_pe, dec_pos, w_ed,
                                 enc_qkv_t, enc_proj2, enc_up, enc_down)
         both = decode(z, rank, dec_pos, pos_x, dec_qkv_t, dec_proj2, dec_up, dec_down)
-        return jnp.einsum('cne,ep->cnp', both, w_out, preferred_element_type=F32)
+        return project(both, w_out)
 
     row_spec = P('dp', 'sp', None)
     pos_spec = P(('dp', 'sp'), None)

time: 155 us -> 146 us (0.942)
  matrix products: 6.42 us -> 0 us
  local copies, waits for them, and re-layouts: 2.64 us -> 0 us
    pallas_call x0 -> x1, Pallas kernels: none -> 7.69 us  [project(): pl.pallas_call(output_kernel, grid=(CLIPS * TOK // OUT_ROWS,), out_shape=...]
    pallas_call x1, Pallas kernels: 43.6 us -> 36.5 us  [encode(): pl.pallas_call(encoder_kernel, out_shape=(jax.ShapeDtypeStruct((ROWS + 2...]
    dot_general x1 -> x0, matrix products: 6.42 us -> none  [local_program(): return jnp.einsum('cne,ep->cnp', both, w_out, preferred_element_type=F32)]
    reshape x2 -> x0, local copies, waits for them, and re-layouts: 2.63 us -> none  [the longest x1 1.37 us: local_program(): mask_token.reshape(1, DDIM)]
where the time goes in v1:
time: 146 us
  Pallas kernels  146 us (100%)
    pallas_call x1, Pallas kernels, decode(): pl.pallas_call(decoder_kernel, out_shape=jax.ShapeDtypeStruct((CLIPS, TOK...  102 us
    pallas_call x1, Pallas kernels, encode(): pl.pallas_call(encoder_kernel, out_shape=(jax.ShapeDtypeStruct((ROWS + 2...  36.5 us
    pallas_call x1, Pallas kernels, project(): pl.pallas_call(output_kernel, grid=(CLIPS * TOK // OUT_ROWS,), out_shape=...  7.69 us

profile of v1, /device:TPU:0, one launch (start us, length us, event | category | flops | bytes accessed | tf_op | source)
XLA Modules:
  0.0 146.0 jit_solution(15206226335532178800)
XLA Ops:
  0.0 36.5 %encoder.1 = (bf16[512,384]{1,0:T(8,128)(2,1)}, s32[8,768]{1,0:T(8,128)}, bf16[3,768,384]{2,1,0:T(8,128)(2,1)}) custom-call(s32[2,768]{1,0:T(2,128)} %mask_ref.1, bf16[768]{0:T(1024)(128)(2,1)} %bpe_ref.1, bf16[384]{0:T(512)(128)(2,1)} %token_ref.1, bf16[2,768,1536]{2,1,0:T(8,128)(2,1)} %patch_hbm.1, bf16[768,768]{1,0:T(8,128)(2,1)} %pos_hbm.1, ...), custom_call_target="tpu_custom_call" | custom-call | flops 12000000000 | bytes 40000000 | tf_op jit(solution)/shard_map/encoder/pallas_call | solution.py:233
  36.5 101.8 %decoder.1 = bf16[2,768,384]{2,1,0:T(8,128)(2,1)} custom-call(bf16[512,384]{1,0:T(8,128)(2,1)} %get-tuple-element.8.z_ref, s32[8,768]{1,0:T(8,128)} %get-tuple-element.9.rank_ref, bf16[768,384]{1,0:T(8,128)(2,1)} %pos_me.1, bf16[3,768,384]{2,1,0:T(8,128)(2,1)} %get-tuple-element.10.pos_x, bf16[2,1152,384]{2,1,0:T(8,128)(2,1)} %bitcast.13, ...), custom_call_target="tpu_custom_call" | custom-call | flops 60000002048 | bytes 20000000 | tf_op jit(solution)/shard_map/decoder/pallas_call | solution.py:481
  138.3 7.7 %output.1 = f32[1536,1536]{1,0:T(8,128)} custom-call(bf16[1536,384]{1,0:T(8,128)(2,1)} %bitcast.10, bf16[384,1536]{1,0:T(8,128)(2,1)} %w_ref.1), custom_call_target="tpu_custom_call" | custom-call | flops 2000000000 | bytes 12000000 | tf_op jit(solution)/shard_map/output/pallas_call | solution.py:523

commit v2 on v1

--- a/solution.py
+++ b/solution.py
@@ -307,13 +307,13 @@
 def make_keys(rows, norm, w_k, w_v, k_n, k_dup, v_t):
     a = norm[rows, :]
     k = dot_nt(a, w_k)
-    k_n[rows, :] = k.astype(BF16)
     first = lax.broadcasted_iota(jnp.int32, (k.shape[0], PAIR), 1) < HEAD
     for pair in range(DEC_HEADS // 2):
         both = k[:, pair * PAIR:(pair + 1) * PAIR]
         turned = pltpu.roll(both, HEAD, axis=1)
-        k_dup[rows, 2 * pair * PAIR:(2 * pair + 1) * PAIR] = jnp.where(first, both, turned).astype(BF16)
-        k_dup[rows, (2 * pair + 1) * PAIR:(2 * pair + 2) * PAIR] = jnp.where(first, turned, both).astype(BF16)
+        k_n[pair, rows, :] = both.astype(BF16)
+        k_dup[2 * pair, rows, :] = jnp.where(first, both, turned).astype(BF16)
+        k_dup[2 * pair + 1, rows, :] = jnp.where(first, turned, both).astype(BF16)
     v_t[:, rows] = dot_nt(w_v, a).astype(BF16)
 
 
@@ -329,8 +329,6 @@
         if unit_q is not None:
             head_q, cols_q = place(unit_q)
             q = q_3[head_q, :, cols_q]
-            lanes = pl.ds(pl.multiple_of((head_q // 2) * PAIR, PAIR), PAIR)
-            lanes_dup = pl.ds(pl.multiple_of(head_q * PAIR, PAIR), PAIR)
         if unit_p is not None:
             head_p, cols_p = place(unit_p)
             shift = col_max(max8)
@@ -352,7 +350,7 @@
                     weigh(*late)
                 late = (idx, e.astype(BF16))
             if unit_q is not None:
-                keys = jnp.concatenate([k_dup[rows, lanes_dup], k_n[rows, lanes]], axis=1)
+                keys = jnp.concatenate([k_dup[head_q, rows, :], k_n[head_q // 2, rows, :]], axis=1)
                 s = dot(keys, q)
                 s_q[rows, :] = s
                 m = jnp.max(s.reshape(K_BLK // 8, 8, Q_BLK), axis=0)
@@ -378,8 +376,8 @@
     return (mid.astype(F32) + dot(act, w_down)).astype(BF16)
 
 
-def decoder_kernel(z_ref, rank_ref, pos_me, pos_x, qkv_hbm, proj_hbm, up_hbm, down_hbm, both_ref,
-                   qkv, proj, up, down, hid, norm, fin, q_3, k_n, k_dup, v_t, o_t, s_even, s_odd, w_sem, ready, row_send, row_recv, fin_send, fin_recv):
+def decoder_kernel(z_ref, rank_ref, pos_me, pos_x, qkv_hbm, proj_hbm, up_hbm, down_hbm, far_ref, hid_out, o_out,
+                   qkv, proj, up, down, hid, norm, fin, q_3, k_n, k_dup, v_t, o_t, s_even, s_odd, w_sem, ready, row_send, row_recv, fin_send, fin_recv, out_sem):
     me = lax.axis_index('sp')
     chip = me // 2
     core = me - 2 * chip
@@ -460,29 +458,49 @@
         row_copy(i).wait()
     keys(1, OWN, OWN)
 
+    keep = pltpu.make_async_copy(hid.at[pl.ds(TOK, TOK)], hid_out, out_sem.at[0])
+    keep.start()
     early = 2 * Q_BLK
     attention(0, early, q_3, k_n, k_dup, v_t, o_t, s_even, s_odd)
-
-    def last_rows(rows):
+    pieces = TOK // CHUNK
+
+    def fin_copy(i):
+        rows = pl.ds(pl.multiple_of(i * CHUNK, CHUNK), CHUNK)
+        return pltpu.make_async_remote_copy(
+            src_ref=fin.at[rows], dst_ref=far_ref.at[rows], send_sem=fin_send.at[i], recv_sem=fin_recv.at[i],
+            device_id={'sp': peer}, device_id_type=MESH)
+
+    def peer_mlp(i, carry):
+        rows = pl.ds(pl.multiple_of(i * CHUNK, CHUNK), CHUNK)
         fin[rows, :] = layer_norm(mlp(rows, hid, o_t, proj[1], up[1], down[1]))
 
-    fill_rows(0, early, CHUNK, last_rows)
-    send = pltpu.make_async_remote_copy(
-        src_ref=fin.at[pl.ds(0, TOK)], dst_ref=both_ref.at[chip], send_sem=fin_send, recv_sem=fin_recv,
-        device_id={'sp': peer}, device_id_type=MESH)
-    send.start()
+        @pl.when(i > 0)
+        def _():
+            fin_copy(i - 1).start()
+
+        return carry
+
+    lax.fori_loop(0, pieces, peer_mlp, 0)
+    fin_copy(pieces - 1).start()
     attention(early, OWN - early, q_3, k_n, k_dup, v_t, o_t, s_even, s_odd)
-    fill_rows(early, OWN - early, CHUNK, last_rows)
-    both_ref[chip] = fin[TOK:OWN]
-    send.wait()
+    give = pltpu.make_async_copy(o_t.at[:, pl.ds(TOK, TOK)], o_out, out_sem.at[1])
+    give.start()
+    for i in range(pieces):
+        fin_copy(i).wait()
+    keep.wait()
+    give.wait()
 
 
 def decode(z, rank, pos, pos_x, wqkv, wproj, wup, wdown):
     return pl.pallas_call(
         decoder_kernel,
-        out_shape=jax.ShapeDtypeStruct((CLIPS, TOK, DDIM), BF16),
+        out_shape=(
+            jax.ShapeDtypeStruct((TOK, DDIM), BF16),
+            jax.ShapeDtypeStruct((TOK, DDIM), BF16),
+            jax.ShapeDtypeStruct((DDIM, TOK), BF16),
+        ),
         in_specs=[VMEM] * 4 + [ANY] * 4,
-        out_specs=VMEM,
+        out_specs=(VMEM, ANY, ANY),
         scratch_shapes=[
             pltpu.VMEM((LAYERS, 3 * DDIM, DDIM), BF16),
             pltpu.VMEM((LAYERS, DDIM, DDIM), BF16),
@@ -490,10 +508,10 @@
             pltpu.VMEM((LAYERS, 4 * DDIM, DDIM), BF16),
             pltpu.VMEM((OWN, DDIM), BF16),
             pltpu.VMEM((SEQ, DDIM), BF16),
-            pltpu.VMEM((OWN, DDIM), BF16),
+            pltpu.VMEM((TOK, DDIM), BF16),
             pltpu.VMEM((DEC_HEADS, 4 * HEAD, OWN), BF16),
-            pltpu.VMEM((SEQ, DDIM), BF16),
-            pltpu.VMEM((SEQ, 2 * DDIM), BF16),
+            pltpu.VMEM((DEC_HEADS // 2, SEQ, PAIR), BF16),
+            pltpu.VMEM((DEC_HEADS, SEQ, PAIR), BF16),
             pltpu.VMEM((DDIM, SEQ), BF16),
             pltpu.VMEM((DDIM, OWN), BF16),
             pltpu.VMEM((SEQ, Q_BLK), F32),
@@ -502,8 +520,9 @@
             pltpu.SemaphoreType.REGULAR,
             pltpu.SemaphoreType.DMA((OWN // CHUNK,)),
             pltpu.SemaphoreType.DMA((OWN // CHUNK,)),
-            pltpu.SemaphoreType.DMA,
-            pltpu.SemaphoreType.DMA,
+            pltpu.SemaphoreType.DMA((TOK // CHUNK,)),
+            pltpu.SemaphoreType.DMA((TOK // CHUNK,)),
+            pltpu.SemaphoreType.DMA((2,)),
         ],
         compiler_params=pltpu.CompilerParams(collective_id=1, has_side_effects=True, vmem_limit_bytes=58 * 2 ** 20),
         cost_estimate=pl.CostEstimate(flops=60 * 10 ** 9, bytes_accessed=2 * 10 ** 7, transcendentals=6 * 10 ** 7),
@@ -511,25 +530,56 @@
     )(z, rank, pos, pos_x, wqkv, wproj, wup, wdown)
 
 
-OUT_ROWS = 256
-
-
-def output_kernel(both_ref, w_ref, out_ref):
-    out_ref[...] = dot(both_ref[...], w_ref[...])
-
-
-def project(both, w_out):
-    rows = both.reshape(CLIPS * TOK, DDIM)
-    out = pl.pallas_call(
+def output_kernel(far_ref, hid, o_t, w_ref, proj_hbm, up_hbm, down_hbm, out_hbm, proj, up, down, buf, w_sem, out_sem):
+    chip = lax.axis_index('sp') // 2
+    loads = [pltpu.make_async_copy(src.at[LAYERS - 1], dst, w_sem.at[idx])
+             for idx, (src, dst) in enumerate(((proj_hbm, proj), (up_hbm, up), (down_hbm, down)))]
+    for copy in loads:
+        copy.start()
+    pieces = TOK // CHUNK
+
+    def out_copy(slot, clip, i):
+        rows = pl.ds(pl.multiple_of(i * CHUNK, CHUNK), CHUNK)
+        return pltpu.make_async_copy(buf.at[slot], out_hbm.at[clip, rows], out_sem.at[slot])
+
+    def far_rows(i, carry):
+        buf[i] = dot(far_ref[pl.ds(pl.multiple_of(i * CHUNK, CHUNK), CHUNK), :], w_ref[...])
+        out_copy(i, 1 - chip, i).start()
+        return carry
+
+    def near_rows(i, carry):
+        rows = pl.ds(pl.multiple_of(i * CHUNK, CHUNK), CHUNK)
+        buf[pieces + i] = dot(layer_norm(mlp(rows, hid, o_t, proj[...], up[...], down[...])), w_ref[...])
+        out_copy(pieces + i, chip, i).start()
+        return carry
+
+    lax.fori_loop(0, pieces, far_rows, 0)
+    for copy in loads:
+        copy.wait()
+    lax.fori_loop(0, pieces, near_rows, 0)
+    for i in range(pieces):
+        out_copy(i, 1 - chip, i).wait()
+        out_copy(pieces + i, chip, i).wait()
+
+
+def project(far, hid, o_t, w_out, proj, up, down):
+    return pl.pallas_call(
         output_kernel,
-        grid=(CLIPS * TOK // OUT_ROWS,),
-        out_shape=jax.ShapeDtypeStruct((CLIPS * TOK, PATCH), F32),
-        in_specs=[pl.BlockSpec((OUT_ROWS, DDIM), lambda i: (i, 0)), pl.BlockSpec((DDIM, PATCH), lambda i: (0, 0))],
-        out_specs=pl.BlockSpec((OUT_ROWS, PATCH), lambda i: (i, 0)),
-        cost_estimate=pl.CostEstimate(flops=2 * 10 ** 9, bytes_accessed=12 * 10 ** 6, transcendentals=0),
+        out_shape=jax.ShapeDtypeStruct((CLIPS, TOK, PATCH), F32),
+        in_specs=[VMEM] * 4 + [ANY] * 3,
+        out_specs=ANY,
+        scratch_shapes=[
+            pltpu.VMEM((DDIM, DDIM), BF16),
+            pltpu.VMEM((DDIM, 4 * DDIM), BF16),
+            pltpu.VMEM((4 * DDIM, DDIM), BF16),
+            pltpu.VMEM((CLIPS * TOK // CHUNK, CHUNK, PATCH), F32),
+            pltpu.SemaphoreType.DMA((3,)),
+            pltpu.SemaphoreType.DMA((CLIPS * TOK // CHUNK,)),
+        ],
+        compiler_params=pltpu.CompilerParams(vmem_limit_bytes=62 * 2 ** 20),
+        cost_estimate=pl.CostEstimate(flops=5 * 10 ** 9, bytes_accessed=15 * 10 ** 6, transcendentals=0),
         name='output',
-    )(rows, w_out)
-    return out.reshape(CLIPS, TOK, PATCH)
+    )(far, hid, o_t, w_out, proj, up, down)
 
 
 def solution(mesh):
@@ -540,8 +590,8 @@
         dec_proj2 = dec_proj.reshape(LAYERS, DDIM, DDIM)
         z, rank, pos_x = encode(vis_mask, b_pe, mask_token, patches, enc_pos, w_pe, dec_pos, w_ed,
                                 enc_qkv_t, enc_proj2, enc_up, enc_down)
-        both = decode(z, rank, dec_pos, pos_x, dec_qkv_t, dec_proj2, dec_up, dec_down)
-        return project(both, w_out)
+        far, hid, o_t = decode(z, rank, dec_pos, pos_x, dec_qkv_t, dec_proj2, dec_up, dec_down)
+        return project(far, hid, o_t, w_out, dec_proj2, dec_up, dec_down)
 
     row_spec = P('dp', 'sp', None)
     pos_spec = P(('dp', 'sp'), None)

time: 146 us -> 146 us (level)
  no operation moved by 1% of the time
where the time goes in v2:
time: 146 us
  Pallas kernels  146 us (100%)
    pallas_call x1, Pallas kernels, decode(): pl.pallas_call(decoder_kernel, out_shape=(jax.ShapeDtypeStruct((TOK, DDIM...  97.6 us
    pallas_call x1, Pallas kernels, encode(): pl.pallas_call(encoder_kernel, out_shape=(jax.ShapeDtypeStruct((ROWS + 2...  36.5 us
    pallas_call x1, Pallas kernels, project(): pl.pallas_call(output_kernel, out_shape=jax.ShapeDtypeStruct((CLIPS, TOK,...  11.9 us

profile of v2, /device:TPU:0, one launch (start us, length us, event | category | flops | bytes accessed | tf_op | source)
XLA Modules:
  0.0 146.2 jit_solution(12619174555099879892)
XLA Ops:
  0.0 36.5 %encoder.1 = (bf16[512,384]{1,0:T(8,128)(2,1)}, s32[8,768]{1,0:T(8,128)}, bf16[3,768,384]{2,1,0:T(8,128)(2,1)}) custom-call(s32[2,768]{1,0:T(2,128)} %mask_ref.1, bf16[768]{0:T(1024)(128)(2,1)} %bpe_ref.1, bf16[384]{0:T(512)(128)(2,1)} %token_ref.1, bf16[2,768,1536]{2,1,0:T(8,128)(2,1)} %patch_hbm.1, bf16[768,768]{1,0:T(8,128)(2,1)} %pos_hbm.1, ...), custom_call_target="tpu_custom_call" | custom-call | flops 12000000000 | bytes 40000000 | tf_op jit(solution)/shard_map/encoder/pallas_call | solution.py:233
  36.5 97.6 %decoder.1 = (bf16[768,384]{1,0:T(8,128)(2,1)}, bf16[768,384]{1,0:T(8,128)(2,1)}, bf16[384,768]{1,0:T(8,128)(2,1)}) custom-call(bf16[512,384]{1,0:T(8,128)(2,1)} %get-tuple-element.11.z_ref, s32[8,768]{1,0:T(8,128)} %get-tuple-element.12.rank_ref, bf16[768,384]{1,0:T(8,128)(2,1)} %pos_me.1, bf16[3,768,384]{2,1,0:T(8,128)(2,1)} %get-tuple-element.13.pos_x, ...), custom_call_target="tpu_custom_call" | custom-call | flops 60000002048 | bytes 20000000 | tf_op jit(solution)/shard_map/decoder/pallas_call | solution.py:495
  134.1 11.9 %output.1 = f32[2,768,1536]{2,1,0:T(8,128)} custom-call(bf16[768,384]{1,0:T(8,128)(2,1)} %get-tuple-element.14.far_ref, bf16[768,384]{1,0:T(8,128)(2,1)} %get-tuple-element.15.hid, bf16[384,768]{1,0:T(8,128)(2,1)} %get-tuple-element.16.o_t, bf16[384,1536]{1,0:T(8,128)(2,1)} %w_ref.1, bf16[2,384,384]{2,1,0:T(8,128)(2,1)} %bitcast.12, ...), custom_call_target="tpu_custom_call" | custom-call | flops 5000000000 | bytes 15000000 | tf_op jit(solution)/shard_map/output/pallas_call | solution.py:566

commit v3 on v2

--- a/solution.py
+++ b/solution.py
@@ -280,6 +280,7 @@
 CHUNK = 256
 WIDE = 512
 PAIR = 2 * HEAD
+MIN_SUM = 2.0 ** -64
 
 
 def fill_rows(start, count, step, body):
@@ -290,84 +291,110 @@
     lax.fori_loop(0, count // step, run, 0)
 
 
-def make_queries(rows, norm, w_q, q_3):
+def make_queries(rows, norm, w_q, q_3, q_sq):
     q = dot_nt(w_q, norm[rows, :]).astype(BF16).astype(F32) * EXP_SCALE
     hi = q.astype(BF16)
     rest = q - hi.astype(F32)
     mid = rest.astype(BF16)
     low = (rest - mid.astype(F32)).astype(BF16)
     zero = jnp.zeros((HEAD, q.shape[1]), BF16)
+    square = q * q
     for head in range(DEC_HEADS):
         part = slice(head * HEAD, (head + 1) * HEAD)
-        tail = (low[part], zero) if head % 2 == 0 else (zero, low[part])
-        for idx, val in enumerate((hi[part], mid[part]) + tail):
+        for idx, val in enumerate((hi[part], mid[part], low[part], zero)):
             q_3[head, idx * HEAD:(idx + 1) * HEAD, rows] = val
-
-
-def make_keys(rows, norm, w_k, w_v, k_n, k_dup, v_t):
+        q_sq[head:head + 1, rows] = col_sum(square[part])
+
+
+def set_shifts(q_3, q_sq, k_sq):
+    for head in range(DEC_HEADS):
+        bound = 1.02 * lax.sqrt(q_sq[head:head + 1, :] * k_sq[0:1, head:head + 1])
+        first = lax.broadcasted_iota(jnp.int32, (16, OWN), 0) == 0
+        q_3[head, 3 * HEAD:3 * HEAD + 16, :] = jnp.where(first, -bound, 0.0).astype(BF16)
+
+
+def make_keys(rows, norm, w_k, w_v, k_one, k_dup, v_t):
     a = norm[rows, :]
-    k = dot_nt(a, w_k)
-    first = lax.broadcasted_iota(jnp.int32, (k.shape[0], PAIR), 1) < HEAD
+    k = dot_nt(a, w_k).astype(BF16).astype(F32)
+    count = k.shape[0]
+    lane = lax.broadcasted_iota(jnp.int32, (count, PAIR), 1)
+    first = lane < HEAD
+    ones = jnp.where(lane == HEAD, 1.0, 0.0)
     for pair in range(DEC_HEADS // 2):
         both = k[:, pair * PAIR:(pair + 1) * PAIR]
         turned = pltpu.roll(both, HEAD, axis=1)
-        k_n[pair, rows, :] = both.astype(BF16)
-        k_dup[2 * pair, rows, :] = jnp.where(first, both, turned).astype(BF16)
-        k_dup[2 * pair + 1, rows, :] = jnp.where(first, turned, both).astype(BF16)
+        for odd, (low, high) in enumerate(((both, turned), (turned, both))):
+            k_dup[2 * pair + odd, rows, :] = jnp.where(first, low, high).astype(BF16)
+            k_one[2 * pair + odd, rows, :] = jnp.where(first, low, ones).astype(BF16)
     v_t[:, rows] = dot_nt(w_v, a).astype(BF16)
-
-
-def attention(start, count, q_3, k_n, k_dup, v_t, o_t, s_even, s_odd):
+    owner = lax.broadcasted_iota(jnp.int32, (DDIM, PAIR), 0) // HEAD
+    pick = jnp.where(owner == lax.broadcasted_iota(jnp.int32, (DDIM, PAIR), 1), 1.0, 0.0).astype(BF16)
+    norms = dot((k * k).astype(BF16), pick) * 1.02
+    return jnp.max(norms.reshape(count // 8, 8, PAIR), axis=0)
+
+
+def attention(start, count, q_3, k_one, k_dup, v_t, o_t, least):
     blocks = count // Q_BLK
-    units = DEC_HEADS * blocks
-
-    def place(unit):
+
+    def body(unit, least):
         head = unit // blocks
-        return head, pl.ds(pl.multiple_of(start + (unit - head * blocks) * Q_BLK, Q_BLK), Q_BLK)
-
-    def mixed(unit_q, s_q, unit_p, s_p, max8):
-        if unit_q is not None:
-            head_q, cols_q = place(unit_q)
-            q = q_3[head_q, :, cols_q]
-        if unit_p is not None:
-            head_p, cols_p = place(unit_p)
-            shift = col_max(max8)
-            v_rows = pl.ds(pl.multiple_of(head_p * HEAD, HEAD), HEAD)
-        new_max = total = late = None
-        accs = [None, None]
-
-        def weigh(idx, weights):
-            o = dot(v_t[v_rows, idx * K_BLK:(idx + 1) * K_BLK], weights)
-            accs[idx % 2] = o if accs[idx % 2] is None else accs[idx % 2] + o
-
+        cols = pl.ds(pl.multiple_of(start + (unit - head * blocks) * Q_BLK, Q_BLK), Q_BLK)
+        q = q_3[head, :, cols]
+        v_rows = pl.ds(pl.multiple_of(head * HEAD, HEAD), HEAD)
+
+        def scores(idx):
+            rows = slice(idx * K_BLK, (idx + 1) * K_BLK)
+            return dot(jnp.concatenate([k_dup[head, rows, :], k_one[head, rows, :]], axis=1), q)
+
+        ahead = scores(0)
+        total = acc = None
         for idx in range(SEQ // K_BLK):
-            rows = slice(idx * K_BLK, (idx + 1) * K_BLK)
-            if unit_p is not None:
-                e = jnp.exp2(s_p[rows, :] - shift)
-                t = jnp.sum(e.reshape(K_BLK // 8, 8, Q_BLK), axis=0)
-                total = t if total is None else total + t
-                if late is not None:
-                    weigh(*late)
-                late = (idx, e.astype(BF16))
-            if unit_q is not None:
-                keys = jnp.concatenate([k_dup[head_q, rows, :], k_n[head_q // 2, rows, :]], axis=1)
-                s = dot(keys, q)
-                s_q[rows, :] = s
-                m = jnp.max(s.reshape(K_BLK // 8, 8, Q_BLK), axis=0)
-                new_max = m if new_max is None else jnp.maximum(new_max, m)
-        if unit_p is not None:
-            weigh(*late)
-            o_t[v_rows, cols_p] = ((accs[0] + accs[1]) * (1.0 / col_sum(total))).astype(BF16)
-        return new_max
-
-    first = mixed(0, s_even, None, None, None)
-
-    def body(i, max8):
-        unit = 2 * i
-        max_odd = mixed(unit + 1, s_odd, unit, s_even, max8)
-        return mixed(jnp.minimum(unit + 2, units - 1), s_even, unit + 1, s_odd, max_odd)
-
-    lax.fori_loop(0, units // 2, body, first)
+            s = ahead
+            if idx + 1 < SEQ // K_BLK:
+                ahead = scores(idx + 1)
+            e = jnp.exp2(s)
+            t = jnp.sum(e.reshape(K_BLK // 8, 8, Q_BLK), axis=0)
+            total = t if total is None else total + t
+            o = dot(v_t[v_rows, idx * K_BLK:(idx + 1) * K_BLK], e.astype(BF16))
+            acc = o if acc is None else acc + o
+        total = col_sum(total)
+        o_t[v_rows, cols] = (acc * (1.0 / total)).astype(BF16)
+        return jnp.where(total >= MIN_SUM, least, 0.0)
+
+    return lax.fori_loop(0, DEC_HEADS * blocks, body, least)
+
+
+X_BLK = 256
+
+
+def attention_exact(start, count, q_3, k_one, k_dup, v_t, o_t, s_buf):
+    blocks = count // X_BLK
+
+    def body(unit, carry):
+        head = unit // blocks
+        cols = pl.ds(pl.multiple_of(start + (unit - head * blocks) * X_BLK, X_BLK), X_BLK)
+        q = q_3[head, :, cols]
+        v_rows = pl.ds(pl.multiple_of(head * HEAD, HEAD), HEAD)
+
+        def measure(i, peak):
+            rows = pl.ds(pl.multiple_of(i * K_BLK, K_BLK), K_BLK)
+            s = dot(jnp.concatenate([k_dup[head, rows, :], k_one[head, rows, :]], axis=1), q)
+            s_buf[rows, :] = s
+            return jnp.maximum(peak, jnp.max(s.reshape(K_BLK // 8, 8, X_BLK), axis=0))
+
+        shift = col_max(lax.fori_loop(0, SEQ // K_BLK, measure, jnp.full((8, X_BLK), -jnp.inf, F32)))
+
+        def weigh(i, sums):
+            rows = pl.ds(pl.multiple_of(i * K_BLK, K_BLK), K_BLK)
+            e = jnp.exp2(s_buf[rows, :] - shift)
+            total = sums[0] + jnp.sum(e.reshape(K_BLK // 8, 8, X_BLK), axis=0)
+            return total, sums[1] + dot(v_t[v_rows, rows], e.astype(BF16))
+
+        total, acc = lax.fori_loop(0, SEQ // K_BLK, weigh, (jnp.zeros((8, X_BLK), F32), jnp.zeros((HEAD, X_BLK), F32)))
+        o_t[v_rows, cols] = (acc * (1.0 / col_sum(total))).astype(BF16)
+        return carry
+
+    lax.fori_loop(0, DEC_HEADS * blocks, body, 0)
 
 
 def mlp(rows, hid, o_t, w_proj, w_up, w_down):
@@ -376,8 +403,8 @@
     return (mid.astype(F32) + dot(act, w_down)).astype(BF16)
 
 
-def decoder_kernel(z_ref, rank_ref, pos_me, pos_x, qkv_hbm, proj_hbm, up_hbm, down_hbm, far_ref, hid_out, o_out,
-                   qkv, proj, up, down, hid, norm, fin, q_3, k_n, k_dup, v_t, o_t, s_even, s_odd, w_sem, ready, row_send, row_recv, fin_send, fin_recv, out_sem):
+def decoder_kernel(exact, z_ref, rank_ref, pos_me, pos_x, qkv_hbm, proj_hbm, up_hbm, down_hbm, far_ref, hid_out, o_out, least_ref,
+                   qkv, proj, up, down, hid, norm, fin, q_3, q_sq, k_sq, k_one, k_dup, v_t, o_t, s_buf, least_mine, least_all, w_sem, least_send, least_recv, ready, row_send, row_recv, fin_send, fin_recv, out_sem):
     me = lax.axis_index('sp')
     chip = me // 2
     core = me - 2 * chip
@@ -392,9 +419,9 @@
             copy.start()
             copies.append(copy)
     barrier = pltpu.get_barrier_semaphore()
-    for other in (peer, sib):
+    for other in (peer, sib, diag):
         pl.semaphore_signal(barrier, inc=1, device_id={'sp': other}, device_id_type=MESH)
-    pl.semaphore_wait(barrier, 2)
+    pl.semaphore_wait(barrier, 3)
 
     def tokens(dev, pos):
         slot = lax.rem(me - dev + SP, SP)
@@ -414,18 +441,36 @@
 
     fill_rows(0, OWN, CHUNK, own_norm)
 
+    wide = CHUNK if exact else WIDE
+
     def queries(layer):
-        fill_rows(0, OWN, WIDE, lambda rows: make_queries(rows, norm, qkv[layer, 0:DDIM], q_3))
+        fill_rows(0, OWN, wide, lambda rows: make_queries(rows, norm, qkv[layer, 0:DDIM], q_3, q_sq))
 
     def keys(layer, start, count):
-        fill_rows(start, count, WIDE, lambda rows: make_keys(
-            rows, norm, qkv[layer, DDIM:2 * DDIM], qkv[layer, 2 * DDIM:3 * DDIM], k_n, k_dup, v_t))
-
+        def run(i, carry):
+            rows = pl.ds(pl.multiple_of(start + i * wide, wide), wide)
+            norms = make_keys(rows, norm, qkv[layer, DDIM:2 * DDIM], qkv[layer, 2 * DDIM:3 * DDIM], k_one, k_dup, v_t)
+            return jnp.maximum(carry, norms)
+
+        return lax.fori_loop(0, count // wide, run, jnp.zeros((8, PAIR), F32))
+
+    def shifts(norms):
+        if not exact:
+            k_sq[...] = jnp.broadcast_to(col_max(norms), (8, PAIR))
+            set_shifts(q_3, q_sq, k_sq)
+
+    def attend(start, count, least):
+        if exact:
+            attention_exact(start, count, q_3, k_one, k_dup, v_t, o_t, s_buf)
+            return least
+        return attention(start, count, q_3, k_one, k_dup, v_t, o_t, least)
+
+    least = jnp.ones((1, Q_BLK), F32)
     copies[0].wait()
     queries(0)
-    keys(0, 0, SEQ)
+    shifts(keys(0, 0, SEQ))
     pl.semaphore_signal(ready, inc=1, device_id={'sp': sib}, device_id_type=MESH)
-    attention(0, OWN, q_3, k_n, k_dup, v_t, o_t, s_even, s_odd)
+    least = attend(0, OWN, least)
     pl.semaphore_wait(ready, 1)
     for copy in copies[1:]:
         copy.wait()
@@ -453,15 +498,15 @@
     lax.fori_loop(0, steps, first_mlp, 0)
     queries(1)
     row_copy(steps - 1).start()
-    keys(1, 0, OWN)
+    norms = keys(1, 0, OWN)
     for i in range(steps):
         row_copy(i).wait()
-    keys(1, OWN, OWN)
+    shifts(jnp.maximum(norms, keys(1, OWN, OWN)))
 
     keep = pltpu.make_async_copy(hid.at[pl.ds(TOK, TOK)], hid_out, out_sem.at[0])
     keep.start()
     early = 2 * Q_BLK
-    attention(0, early, q_3, k_n, k_dup, v_t, o_t, s_even, s_odd)
+    least = attend(0, early, least)
     pieces = TOK // CHUNK
 
     def fin_copy(i):
@@ -482,25 +527,41 @@
 
     lax.fori_loop(0, pieces, peer_mlp, 0)
     fin_copy(pieces - 1).start()
-    attention(early, OWN - early, q_3, k_n, k_dup, v_t, o_t, s_even, s_odd)
+    least = attend(early, OWN - early, least)
+    least_mine[...] = jnp.broadcast_to(jnp.min(least, axis=1, keepdims=True), (8, PAIR))
+    shares = []
+    for step in range(1, SP):
+        share = pltpu.make_async_remote_copy(
+            src_ref=least_mine, dst_ref=least_all.at[step - 1], send_sem=least_send.at[step - 1], recv_sem=least_recv.at[step - 1],
+            device_id={'sp': lax.rem(me + step, SP)}, device_id_type=MESH)
+        shares.append(share)
     give = pltpu.make_async_copy(o_t.at[:, pl.ds(TOK, TOK)], o_out, out_sem.at[1])
     give.start()
+    for share in shares:
+        share.start()
     for i in range(pieces):
         fin_copy(i).wait()
+    for share in shares:
+        share.wait()
+    low = least_mine[...]
+    for k in range(SP - 1):
+        low = low * least_all[k]
+    least_ref[...] = low
     keep.wait()
     give.wait()
 
 
-def decode(z, rank, pos, pos_x, wqkv, wproj, wup, wdown):
+def decode(exact, z, rank, pos, pos_x, wqkv, wproj, wup, wdown):
     return pl.pallas_call(
-        decoder_kernel,
+        functools.partial(decoder_kernel, exact),
         out_shape=(
             jax.ShapeDtypeStruct((TOK, DDIM), BF16),
             jax.ShapeDtypeStruct((TOK, DDIM), BF16),
             jax.ShapeDtypeStruct((DDIM, TOK), BF16),
+            jax.ShapeDtypeStruct((8, PAIR), F32),
         ),
         in_specs=[VMEM] * 4 + [ANY] * 4,
-        out_specs=(VMEM, ANY, ANY),
+        out_specs=(VMEM, ANY, ANY, VMEM),
         scratch_shapes=[
             pltpu.VMEM((LAYERS, 3 * DDIM, DDIM), BF16),
             pltpu.VMEM((LAYERS, DDIM, DDIM), BF16),
@@ -510,13 +571,18 @@
             pltpu.VMEM((SEQ, DDIM), BF16),
             pltpu.VMEM((TOK, DDIM), BF16),
             pltpu.VMEM((DEC_HEADS, 4 * HEAD, OWN), BF16),
-            pltpu.VMEM((DEC_HEADS // 2, SEQ, PAIR), BF16),
+            pltpu.VMEM((8, OWN), F32),
+            pltpu.VMEM((8, PAIR), F32),
+            pltpu.VMEM((DEC_HEADS, SEQ, PAIR), BF16),
             pltpu.VMEM((DEC_HEADS, SEQ, PAIR), BF16),
             pltpu.VMEM((DDIM, SEQ), BF16),
             pltpu.VMEM((DDIM, OWN), BF16),
-            pltpu.VMEM((SEQ, Q_BLK), F32),
-            pltpu.VMEM((SEQ, Q_BLK), F32),
+            pltpu.VMEM((SEQ if exact else 8, X_BLK), F32),
+            pltpu.VMEM((8, PAIR), F32),
+            pltpu.VMEM((SP - 1, 8, PAIR), F32),
             pltpu.SemaphoreType.DMA((LAYERS * 4,)),
+            pltpu.SemaphoreType.DMA((SP - 1,)),
+            pltpu.SemaphoreType.DMA((SP - 1,)),
             pltpu.SemaphoreType.REGULAR,
             pltpu.SemaphoreType.DMA((OWN // CHUNK,)),
             pltpu.SemaphoreType.DMA((OWN // CHUNK,)),
@@ -524,9 +590,9 @@
             pltpu.SemaphoreType.DMA((TOK // CHUNK,)),
             pltpu.SemaphoreType.DMA((2,)),
         ],
-        compiler_params=pltpu.CompilerParams(collective_id=1, has_side_effects=True, vmem_limit_bytes=58 * 2 ** 20),
+        compiler_params=pltpu.CompilerParams(collective_id=2 if exact else 1, has_side_effects=True, vmem_limit_bytes=58 * 2 ** 20),
         cost_estimate=pl.CostEstimate(flops=60 * 10 ** 9, bytes_accessed=2 * 10 ** 7, transcendentals=6 * 10 ** 7),
-        name='decoder',
+        name='decoder_exact' if exact else 'decoder',
     )(z, rank, pos, pos_x, wqkv, wproj, wup, wdown)
 
 
@@ -590,7 +656,10 @@
         dec_proj2 = dec_proj.reshape(LAYERS, DDIM, DDIM)
         z, rank, pos_x = encode(vis_mask, b_pe, mask_token, patches, enc_pos, w_pe, dec_pos, w_ed,
                                 enc_qkv_t, enc_proj2, enc_up, enc_down)
-        far, hid, o_t = decode(z, rank, dec_pos, pos_x, dec_qkv_t, dec_proj2, dec_up, dec_down)
+        args = (z, rank, dec_pos, pos_x, dec_qkv_t, dec_proj2, dec_up, dec_down)
+        far, hid, o_t, least = decode(False, *args)
+        far, hid, o_t = lax.cond(
+            least[0, 0] > 0.5, lambda near, _: near, lambda _, full: tuple(decode(True, *full)[:3]), (far, hid, o_t), args)
         return project(far, hid, o_t, w_out, dec_proj2, dec_up, dec_down)
 
     row_spec = P('dp', 'sp', None)

time: 146 us -> 162 us (1.11)
  Pallas kernels: 146 us -> 159 us
    pallas_call x1, Pallas kernels: 97.6 us -> 110 us  [decode(): pl.pallas_call(functools.partial(decoder_kernel, exact), out_shape=(jax.S...]
where the time goes in v3:
time: 162 us; the launch traced here: 161 us
  Pallas kernels  159 us (98%)
    pallas_call x1, Pallas kernels, decode(): pl.pallas_call(functools.partial(decoder_kernel, exact), out_shape=(jax.S...  110 us
    pallas_call x1, Pallas kernels, encode(): pl.pallas_call(encoder_kernel, out_shape=(jax.ShapeDtypeStruct((ROWS + 2...  37.3 us
    pallas_call x1, Pallas kernels, project(): pl.pallas_call(output_kernel, out_shape=jax.ShapeDtypeStruct((CLIPS, TOK,...  11.6 us

profile of v3, /device:TPU:0, one launch (start us, length us, event | category | flops | bytes accessed | tf_op | source)
XLA Modules:
  0.0 161.3 jit_solution(12191654916356234199)
XLA Ops:
  0.0 0.0 copy-start
  0.0 0.0 copy-start.1
  0.0 0.0 copy-start.2
  0.0 0.0 copy-start.3
  0.0 37.3 %encoder.1 = (bf16[512,384]{1,0:T(8,128)(2,1)}, s32[8,768]{1,0:T(8,128)S(1)}, bf16[3,768,384]{2,1,0:T(8,128)(2,1)}) custom-call(s32[2,768]{1,0:T(2,128)} %mask_ref.1, bf16[768]{0:T(1024)(128)(2,1)} %bpe_ref.1, bf16[384]{0:T(512)(128)(2,1)} %token_ref.1, bf16[2,768,1536]{2,1,0:T(8,128)(2,1)} %patch_hbm.1, bf16[768,768]{1,0:T(8,128)(2,1)} %pos_hbm.1, ...), custom_call_target="tpu_custom_call" | custom-call | flops 12000000000 | bytes 40000000 | tf_op jit(solution)/shard_map/encoder/pallas_call | solution.py:233
  37.3 0.0 copy-done
  37.3 0.0 copy-done.1
  37.4 0.0 copy-done.2
  37.4 0.0 copy-done.3
  37.4 110.3 %decoder.1 = (bf16[768,384]{1,0:T(8,128)(2,1)}, bf16[768,384]{1,0:T(8,128)(2,1)}, bf16[384,768]{1,0:T(8,128)(2,1)}, f32[8,128]{1,0:T(8,128)}) custom-call(bf16[512,384]{1,0:T(8,128)(2,1)} %get-tuple-element.48.z_ref, s32[8,768]{1,0:T(8,128)S(1)} %get-tuple-element.49.rank_ref, bf16[768,384]{1,0:T(8,128)(2,1)S(1)} %copy-done.2, ...), custom_call_target="tpu_custom_call" | custom-call | flops 60000002048 | bytes 20000000 | tf_op jit(solution)/shard_map/decoder/pallas_call | solution.py:555
  147.7 1.2 slice.3
  149.5 11.6 %output.1 = f32[2,768,1536]{2,1,0:T(8,128)} custom-call(bf16[768,384]{1,0:T(8,128)(2,1)} %get-tuple-element.55.far_ref, bf16[768,384]{1,0:T(8,128)(2,1)} %get-tuple-element.56.hid, bf16[384,768]{1,0:T(8,128)(2,1)} %get-tuple-element.57.o_t, bf16[384,1536]{1,0:T(8,128)(2,1)} %w_ref.1, bf16[2,384,384]{2,1,0:T(8,128)(2,1)S(1)} %bitcast.15, ...), custom_call_target="tpu_custom_call" | custom-call | flops 5000000000 | bytes 15000000 | tf_op jit(solution)/shard_map/output/pallas_call | solution.py:632
  (1 shorter events, 0.0 us)
Async XLA Ops:
  0.0 37.3 %copy-start = (bf16[2,384,1536]{2,1,0:T(8,128)(2,1)S(1)}, bf16[2,384,1536]{2,1,0:T(8,128)(2,1)}, u32[]{:S(2)}) copy-start(bf16[2,384,1536]{2,1,0:T(8,128)(2,1)} %up_hbm.5) | copy-start | bytes 7077892
  0.0 37.3 %copy-start.1 = (bf16[2,1536,384]{2,1,0:T(8,128)(2,1)S(1)}, bf16[2,1536,384]{2,1,0:T(8,128)(2,1)}, u32[]{:S(2)}) copy-start(bf16[2,1536,384]{2,1,0:T(8,128)(2,1)} %down_hbm.5) | copy-start | bytes 7077892
  0.0 37.4 %copy-start.2 = (bf16[768,384]{1,0:T(8,128)(2,1)S(1)}, bf16[768,384]{1,0:T(8,128)(2,1)}, u32[]{:S(2)}) copy-start(bf16[768,384]{1,0:T(8,128)(2,1)} %pos_me.1) | copy-start | bytes 1769476
  0.0 37.4 %copy-start.3 = (bf16[2,6,64,384]{3,2,1,0:T(8,128)(2,1)S(1)}, bf16[2,6,64,384]{3,2,1,0:T(8,128)(2,1)}, u32[]{:S(2)}) copy-start(bf16[2,6,64,384]{3,2,1,0:T(8,128)(2,1)} %param.32) | copy-start | bytes 1769476

commit v4 on v1

--- a/solution.py
+++ b/solution.py
@@ -78,8 +78,9 @@
     sib = me + 1 - 2 * core
     diag = lax.rem(sib + 2, SP)
 
+    near_load = pltpu.make_async_copy(patch_hbm.at[chip], patch.at[chip], in_sem.at[3])
     loads = [pltpu.make_async_copy(src, dst, in_sem.at[idx])
-             for idx, (src, dst) in enumerate(((patch_hbm, patch), (wpe_hbm, wpe), (pos_hbm, pos)))]
+             for idx, (src, dst) in enumerate(((patch_hbm.at[1 - chip], patch.at[1 - chip]), (wpe_hbm, wpe), (pos_hbm, pos)))]
     for copy in loads:
         copy.start()
     barrier = pltpu.get_barrier_semaphore()
@@ -103,6 +104,7 @@
                    for step in range(1, SP)]
     for copy in loads:
         copy.wait()
+    near_load.start()
     copies = []
     for layer in range(LAYERS):
         for idx, (src, dst) in enumerate(((qkv_hbm, qkv), (proj_hbm, proj), (up_hbm, up), (down_hbm, down))):
@@ -125,6 +127,7 @@
     near = jnp.where(chip == 0, slot_of[0:1], slot_of[1:2])
     sendbuf[...] = window(1 - chip, far)
     to_peer = send(sendbuf, win.at[1], win_send.at[0], win_recv.at[0], peer)
+    near_load.wait()
     win[0] = window(chip, near)
     to_sib = send(win.at[0], win.at[2], win_send.at[1], win_recv.at[1], sib)
 
@@ -258,7 +261,7 @@
             pltpu.VMEM((ROWS, DIM), BF16),
             pltpu.VMEM((DIM, ROWS), BF16),
             pltpu.VMEM((DIM, Q_PAD), BF16),
-            pltpu.SemaphoreType.DMA((3,)),
+            pltpu.SemaphoreType.DMA((4,)),
             pltpu.SemaphoreType.DMA((LAYERS * 4,)),
             pltpu.SemaphoreType.DMA((SP - 1,)),
             pltpu.SemaphoreType.DMA((SP - 1,)),
@@ -275,7 +278,7 @@
     )(mask, bpe, token, patches, enc_pos, wpe, dec_pos, wed, qkv_t, proj, up, down)
 
 
-Q_BLK = 512
+Q_BLK = 256
 K_BLK = 256
 CHUNK = 256
 WIDE = 512
@@ -307,13 +310,13 @@
 def make_keys(rows, norm, w_k, w_v, k_n, k_dup, v_t):
     a = norm[rows, :]
     k = dot_nt(a, w_k)
-    k_n[rows, :] = k.astype(BF16)
     first = lax.broadcasted_iota(jnp.int32, (k.shape[0], PAIR), 1) < HEAD
     for pair in range(DEC_HEADS // 2):
         both = k[:, pair * PAIR:(pair + 1) * PAIR]
         turned = pltpu.roll(both, HEAD, axis=1)
-        k_dup[rows, 2 * pair * PAIR:(2 * pair + 1) * PAIR] = jnp.where(first, both, turned).astype(BF16)
-        k_dup[rows, (2 * pair + 1) * PAIR:(2 * pair + 2) * PAIR] = jnp.where(first, turned, both).astype(BF16)
+        k_n[pair, rows, :] = both.astype(BF16)
+        k_dup[2 * pair, rows, :] = jnp.where(first, both, turned).astype(BF16)
+        k_dup[2 * pair + 1, rows, :] = jnp.where(first, turned, both).astype(BF16)
     v_t[:, rows] = dot_nt(w_v, a).astype(BF16)
 
 
@@ -329,37 +332,27 @@
         if unit_q is not None:
             head_q, cols_q = place(unit_q)
             q = q_3[head_q, :, cols_q]
-            lanes = pl.ds(pl.multiple_of((head_q // 2) * PAIR, PAIR), PAIR)
-            lanes_dup = pl.ds(pl.multiple_of(head_q * PAIR, PAIR), PAIR)
         if unit_p is not None:
             head_p, cols_p = place(unit_p)
             shift = col_max(max8)
             v_rows = pl.ds(pl.multiple_of(head_p * HEAD, HEAD), HEAD)
-        new_max = total = late = None
-        accs = [None, None]
-
-        def weigh(idx, weights):
-            o = dot(v_t[v_rows, idx * K_BLK:(idx + 1) * K_BLK], weights)
-            accs[idx % 2] = o if accs[idx % 2] is None else accs[idx % 2] + o
-
+        new_max = total = acc = None
         for idx in range(SEQ // K_BLK):
             rows = slice(idx * K_BLK, (idx + 1) * K_BLK)
             if unit_p is not None:
                 e = jnp.exp2(s_p[rows, :] - shift)
                 t = jnp.sum(e.reshape(K_BLK // 8, 8, Q_BLK), axis=0)
                 total = t if total is None else total + t
-                if late is not None:
-                    weigh(*late)
-                late = (idx, e.astype(BF16))
+                o = dot(v_t[v_rows, rows], e.astype(BF16))
+                acc = o if acc is None else acc + o
             if unit_q is not None:
-                keys = jnp.concatenate([k_dup[rows, lanes_dup], k_n[rows, lanes]], axis=1)
+                keys = jnp.concatenate([k_dup[head_q, rows, :], k_n[head_q // 2, rows, :]], axis=1)
                 s = dot(keys, q)
                 s_q[rows, :] = s
                 m = jnp.max(s.reshape(K_BLK // 8, 8, Q_BLK), axis=0)
                 new_max = m if new_max is None else jnp.maximum(new_max, m)
         if unit_p is not None:
-            weigh(*late)
-            o_t[v_rows, cols_p] = ((accs[0] + accs[1]) * (1.0 / col_sum(total))).astype(BF16)
+            o_t[v_rows, cols_p] = (acc * (1.0 / col_sum(total))).astype(BF16)
         return new_max
 
     first = mixed(0, s_even, None, None, None)
@@ -379,7 +372,7 @@
 
 
 def decoder_kernel(z_ref, rank_ref, pos_me, pos_x, qkv_hbm, proj_hbm, up_hbm, down_hbm, both_ref,
-                   qkv, proj, up, down, hid, norm, fin, q_3, k_n, k_dup, v_t, o_t, s_even, s_odd, w_sem, ready, row_send, row_recv, fin_send, fin_recv):
+                   qkv, proj, up, down, hid, norm, fin, q_3, k_n, k_dup, v_t, o_t, s_even, s_odd, w_sem, ready, row_send, row_recv, fin_send, fin_recv, pos, pos_sem):
     me = lax.axis_index('sp')
     chip = me // 2
     core = me - 2 * chip
@@ -387,6 +380,10 @@
     sib = me + 1 - 2 * core
     diag = lax.rem(sib + 2, SP)
 
+    fetch = [pltpu.make_async_copy(src, pos.at[idx], pos_sem.at[idx])
+             for idx, src in enumerate((pos_me, pos_x.at[0], pos_x.at[1], pos_x.at[2]))]
+    for copy in fetch:
+        copy.start()
     copies = []
     for layer in range(LAYERS):
         for idx, (src, dst) in enumerate(((qkv_hbm, qkv), (proj_hbm, proj), (up_hbm, up), (down_hbm, down))):
@@ -398,18 +395,19 @@
         pl.semaphore_signal(barrier, inc=1, device_id={'sp': other}, device_id_type=MESH)
     pl.semaphore_wait(barrier, 2)
 
-    def tokens(dev, pos):
+    def tokens(dev, idx):
         slot = lax.rem(me - dev + SP, SP)
         rank = rank_ref[pl.ds(2 * slot + chip, 1), :]
         rank_col = jnp.transpose(jnp.broadcast_to(rank.astype(F32), (8, TOK)))[:, 0:1]
         lanes = lax.broadcasted_iota(jnp.int32, (TOK, ROWS + 2 * HEAD), 1).astype(F32)
         select = jnp.where(lanes == rank_col, 1.0, 0.0).astype(BF16)
-        return (dot(select, z_ref[...]) + pos.astype(F32)).astype(BF16)
-
-    hid[0:TOK] = tokens(peer, pos_x[0])
-    hid[TOK:OWN] = tokens(me, pos_me[...])
-    norm[OWN:OWN + TOK] = layer_norm(tokens(diag, pos_x[2]))
-    norm[OWN + TOK:SEQ] = layer_norm(tokens(sib, pos_x[1]))
+        fetch[idx].wait()
+        return (dot(select, z_ref[...]) + pos[idx].astype(F32)).astype(BF16)
+
+    hid[0:TOK] = tokens(peer, 1)
+    hid[TOK:OWN] = tokens(me, 0)
+    norm[OWN:OWN + TOK] = layer_norm(tokens(diag, 3))
+    norm[OWN + TOK:SEQ] = layer_norm(tokens(sib, 2))
 
     def own_norm(rows):
         norm[rows, :] = layer_norm(hid[rows, :])
@@ -460,28 +458,42 @@
         row_copy(i).wait()
     keys(1, OWN, OWN)
 
-    early = 2 * Q_BLK
-    attention(0, early, q_3, k_n, k_dup, v_t, o_t, s_even, s_odd)
-
-    def last_rows(rows):
-        fin[rows, :] = layer_norm(mlp(rows, hid, o_t, proj[1], up[1], down[1]))
-
-    fill_rows(0, early, CHUNK, last_rows)
-    send = pltpu.make_async_remote_copy(
-        src_ref=fin.at[pl.ds(0, TOK)], dst_ref=both_ref.at[chip], send_sem=fin_send, recv_sem=fin_recv,
-        device_id={'sp': peer}, device_id_type=MESH)
-    send.start()
-    attention(early, OWN - early, q_3, k_n, k_dup, v_t, o_t, s_even, s_odd)
-    fill_rows(early, OWN - early, CHUNK, last_rows)
-    both_ref[chip] = fin[TOK:OWN]
-    send.wait()
+    attention(0, TOK, q_3, k_n, k_dup, v_t, o_t, s_even, s_odd)
+    pieces = TOK // CHUNK
+
+    def fin_copy(i):
+        rows = pl.ds(pl.multiple_of(i * CHUNK, CHUNK), CHUNK)
+        return pltpu.make_async_remote_copy(
+            src_ref=fin.at[rows], dst_ref=both_ref.at[chip, rows], send_sem=fin_send.at[i], recv_sem=fin_recv.at[i],
+            device_id={'sp': peer}, device_id_type=MESH)
+
+    def last_mlp(i, carry, start):
+        src = pl.ds(pl.multiple_of(start + i * CHUNK, CHUNK), CHUNK)
+        rows = pl.ds(pl.multiple_of(i * CHUNK, CHUNK), CHUNK)
+        val = layer_norm(mlp(src, hid, o_t, proj[1], up[1], down[1]))
+        if start == 0:
+            fin[rows, :] = val
+
+            @pl.when(i > 0)
+            def _():
+                fin_copy(i - 1).start()
+        else:
+            both_ref[chip, rows, :] = val
+        return carry
+
+    lax.fori_loop(0, pieces, functools.partial(last_mlp, start=0), 0)
+    fin_copy(pieces - 1).start()
+    attention(TOK, TOK, q_3, k_n, k_dup, v_t, o_t, s_even, s_odd)
+    lax.fori_loop(0, pieces, functools.partial(last_mlp, start=TOK), 0)
+    for i in range(pieces):
+        fin_copy(i).wait()
 
 
 def decode(z, rank, pos, pos_x, wqkv, wproj, wup, wdown):
     return pl.pallas_call(
         decoder_kernel,
         out_shape=jax.ShapeDtypeStruct((CLIPS, TOK, DDIM), BF16),
-        in_specs=[VMEM] * 4 + [ANY] * 4,
+        in_specs=[VMEM] * 2 + [ANY] * 6,
         out_specs=VMEM,
         scratch_shapes=[
             pltpu.VMEM((LAYERS, 3 * DDIM, DDIM), BF16),
@@ -490,10 +502,10 @@
             pltpu.VMEM((LAYERS, 4 * DDIM, DDIM), BF16),
             pltpu.VMEM((OWN, DDIM), BF16),
             pltpu.VMEM((SEQ, DDIM), BF16),
-            pltpu.VMEM((OWN, DDIM), BF16),
+            pltpu.VMEM((TOK, DDIM), BF16),
             pltpu.VMEM((DEC_HEADS, 4 * HEAD, OWN), BF16),
-            pltpu.VMEM((SEQ, DDIM), BF16),
-            pltpu.VMEM((SEQ, 2 * DDIM), BF16),
+            pltpu.VMEM((DEC_HEADS // 2, SEQ, PAIR), BF16),
+            pltpu.VMEM((DEC_HEADS, SEQ, PAIR), BF16),
             pltpu.VMEM((DDIM, SEQ), BF16),
             pltpu.VMEM((DDIM, OWN), BF16),
             pltpu.VMEM((SEQ, Q_BLK), F32),
@@ -502,8 +514,10 @@
             pltpu.SemaphoreType.REGULAR,
             pltpu.SemaphoreType.DMA((OWN // CHUNK,)),
             pltpu.SemaphoreType.DMA((OWN // CHUNK,)),
-            pltpu.SemaphoreType.DMA,
-            pltpu.SemaphoreType.DMA,
+            pltpu.SemaphoreType.DMA((TOK // CHUNK,)),
+            pltpu.SemaphoreType.DMA((TOK // CHUNK,)),
+            pltpu.VMEM((SP, TOK, DDIM), BF16),
+            pltpu.SemaphoreType.DMA((SP,)),
         ],
         compiler_params=pltpu.CompilerParams(collective_id=1, has_side_effects=True, vmem_limit_bytes=58 * 2 ** 20),
         cost_estimate=pl.CostEstimate(flops=60 * 10 ** 9, bytes_accessed=2 * 10 ** 7, transcendentals=6 * 10 ** 7),
@@ -511,25 +525,40 @@
     )(z, rank, pos, pos_x, wqkv, wproj, wup, wdown)
 
 
-OUT_ROWS = 256
-
-
-def output_kernel(both_ref, w_ref, out_ref):
-    out_ref[...] = dot(both_ref[...], w_ref[...])
+def output_kernel(both_ref, w_ref, out_hbm, buf, sem):
+    pieces = TOK // CHUNK
+
+    def out_copy(i):
+        clip = i // pieces
+        rows = pl.ds(pl.multiple_of((i - clip * pieces) * CHUNK, CHUNK), CHUNK)
+        return pltpu.make_async_copy(buf.at[i], out_hbm.at[clip, rows], sem.at[i])
+
+    def body(i, carry):
+        clip = i // pieces
+        rows = pl.ds(pl.multiple_of((i - clip * pieces) * CHUNK, CHUNK), CHUNK)
+        buf[i] = dot(both_ref[clip, rows, :], w_ref[...])
+        out_copy(i).start()
+        return carry
+
+    lax.fori_loop(0, CLIPS * pieces, body, 0)
+    for i in range(CLIPS * pieces):
+        out_copy(i).wait()
 
 
 def project(both, w_out):
-    rows = both.reshape(CLIPS * TOK, DDIM)
-    out = pl.pallas_call(
+    return pl.pallas_call(
         output_kernel,
-        grid=(CLIPS * TOK // OUT_ROWS,),
-        out_shape=jax.ShapeDtypeStruct((CLIPS * TOK, PATCH), F32),
-        in_specs=[pl.BlockSpec((OUT_ROWS, DDIM), lambda i: (i, 0)), pl.BlockSpec((DDIM, PATCH), lambda i: (0, 0))],
-        out_specs=pl.BlockSpec((OUT_ROWS, PATCH), lambda i: (i, 0)),
+        out_shape=jax.ShapeDtypeStruct((CLIPS, TOK, PATCH), F32),
+        in_specs=[VMEM] * 2,
+        out_specs=ANY,
+        scratch_shapes=[
+            pltpu.VMEM((CLIPS * TOK // CHUNK, CHUNK, PATCH), F32),
+            pltpu.SemaphoreType.DMA((CLIPS * TOK // CHUNK,)),
+        ],
+        compiler_params=pltpu.CompilerParams(vmem_limit_bytes=62 * 2 ** 20),
         cost_estimate=pl.CostEstimate(flops=2 * 10 ** 9, bytes_accessed=12 * 10 ** 6, transcendentals=0),
         name='output',
-    )(rows, w_out)
-    return out.reshape(CLIPS, TOK, PATCH)
+    )(both, w_out)
 
 
 def solution(mesh):

time: 146 us -> 147 us (level)
    pallas_call x1, Pallas kernels: 102 us -> 105 us  [decode(): pl.pallas_call(decoder_kernel, out_shape=jax.ShapeDtypeStruct((CLIPS, TOK...]
where the time goes in v4:
time: 147 us
  Pallas kernels  147 us (100%)
    pallas_call x1, Pallas kernels, decode(): pl.pallas_call(decoder_kernel, out_shape=jax.ShapeDtypeStruct((CLIPS, TOK...  105 us
    pallas_call x1, Pallas kernels, encode(): pl.pallas_call(encoder_kernel, out_shape=(jax.ShapeDtypeStruct((ROWS + 2...  35.9 us
    pallas_call x1, Pallas kernels, project(): pl.pallas_call(output_kernel, out_shape=jax.ShapeDtypeStruct((CLIPS, TOK,...  6.26 us

profile of v4, /device:TPU:0, one launch (start us, length us, event | category | flops | bytes accessed | tf_op | source)
XLA Modules:
  0.0 146.9 jit_solution(14243343795469873139)
XLA Ops:
  0.0 35.9 %encoder.1 = (bf16[512,384]{1,0:T(8,128)(2,1)}, s32[8,768]{1,0:T(8,128)}, bf16[3,768,384]{2,1,0:T(8,128)(2,1)}) custom-call(s32[2,768]{1,0:T(2,128)} %mask_ref.1, bf16[768]{0:T(1024)(128)(2,1)} %bpe_ref.1, bf16[384]{0:T(512)(128)(2,1)} %token_ref.1, bf16[2,768,1536]{2,1,0:T(8,128)(2,1)} %patch_hbm.1, bf16[768,768]{1,0:T(8,128)(2,1)} %pos_hbm.1, ...), custom_call_target="tpu_custom_call" | custom-call | flops 12000000000 | bytes 40000000 | tf_op jit(solution)/shard_map/encoder/pallas_call | solution.py:236
  35.9 104.6 %decoder.1.both_ref = bf16[2,768,384]{2,1,0:T(8,128)(2,1)} custom-call(bf16[512,384]{1,0:T(8,128)(2,1)} %get-tuple-element.8.z_ref, s32[8,768]{1,0:T(8,128)} %get-tuple-element.9.rank_ref, bf16[768,384]{1,0:T(8,128)(2,1)} %pos_me.1, bf16[3,768,384]{2,1,0:T(8,128)(2,1)} %get-tuple-element.10.pos_x, bf16[2,1152,384]{2,1,0:T(8,128)(2,1)} %bitcast.10, ...), custom_call_target="tpu_custom_call" | custom-call | flops 60000002048 | bytes 20000000 | tf_op jit(solution)/shard_map/decoder/pallas_call | solution.py:493
  140.5 6.3 %output.1 = f32[2,768,1536]{2,1,0:T(8,128)} custom-call(bf16[2,768,384]{2,1,0:T(8,128)(2,1)} %decoder.1.both_ref, bf16[384,1536]{1,0:T(8,128)(2,1)} %w_ref.1), custom_call_target="tpu_custom_call" | custom-call | flops 2000000000 | bytes 12000000 | tf_op jit(solution)/shard_map/output/pallas_call | solution.py:549

commit v5 on v4

--- a/solution.py
+++ b/solution.py
@@ -293,34 +293,25 @@
     lax.fori_loop(0, count // step, run, 0)
 
 
-def make_queries(rows, norm, w_q, q_3):
-    q = dot_nt(w_q, norm[rows, :]).astype(BF16).astype(F32) * EXP_SCALE
-    hi = q.astype(BF16)
-    rest = q - hi.astype(F32)
-    mid = rest.astype(BF16)
-    low = (rest - mid.astype(F32)).astype(BF16)
+def make_queries(rows, norm, w_q, q_z):
+    q = dot_nt(w_q, norm[rows, :]).astype(BF16)
     zero = jnp.zeros((HEAD, q.shape[1]), BF16)
     for head in range(DEC_HEADS):
-        part = slice(head * HEAD, (head + 1) * HEAD)
-        tail = (low[part], zero) if head % 2 == 0 else (zero, low[part])
-        for idx, val in enumerate((hi[part], mid[part]) + tail):
-            q_3[head, idx * HEAD:(idx + 1) * HEAD, rows] = val
-
-
-def make_keys(rows, norm, w_k, w_v, k_n, k_dup, v_t):
+        q_head = q[head * HEAD:(head + 1) * HEAD]
+        low, high = (q_head, zero) if head % 2 == 0 else (zero, q_head)
+        q_z[head, 0:HEAD, rows] = low
+        q_z[head, HEAD:PAIR, rows] = high
+
+
+def make_keys(rows, norm, w_k, w_v, k_n, v_t):
     a = norm[rows, :]
-    k = dot_nt(a, w_k)
-    first = lax.broadcasted_iota(jnp.int32, (k.shape[0], PAIR), 1) < HEAD
+    k = dot_nt(a, w_k).astype(BF16)
     for pair in range(DEC_HEADS // 2):
-        both = k[:, pair * PAIR:(pair + 1) * PAIR]
-        turned = pltpu.roll(both, HEAD, axis=1)
-        k_n[pair, rows, :] = both.astype(BF16)
-        k_dup[2 * pair, rows, :] = jnp.where(first, both, turned).astype(BF16)
-        k_dup[2 * pair + 1, rows, :] = jnp.where(first, turned, both).astype(BF16)
+        k_n[pair, rows, :] = k[:, pair * PAIR:(pair + 1) * PAIR]
     v_t[:, rows] = dot_nt(w_v, a).astype(BF16)
 
 
-def attention(start, count, q_3, k_n, k_dup, v_t, o_t, s_even, s_odd):
+def attention(start, count, q_z, k_n, v_t, o_t, s_even, s_odd):
     blocks = count // Q_BLK
     units = DEC_HEADS * blocks
 
@@ -331,23 +322,22 @@
     def mixed(unit_q, s_q, unit_p, s_p, max8):
         if unit_q is not None:
             head_q, cols_q = place(unit_q)
-            q = q_3[head_q, :, cols_q]
+            q = q_z[head_q, :, cols_q]
         if unit_p is not None:
             head_p, cols_p = place(unit_p)
-            shift = col_max(max8)
+            shift = col_max(max8) * EXP_SCALE
             v_rows = pl.ds(pl.multiple_of(head_p * HEAD, HEAD), HEAD)
         new_max = total = acc = None
         for idx in range(SEQ // K_BLK):
             rows = slice(idx * K_BLK, (idx + 1) * K_BLK)
             if unit_p is not None:
-                e = jnp.exp2(s_p[rows, :] - shift)
+                e = jnp.exp2(s_p[rows, :] * EXP_SCALE - shift)
                 t = jnp.sum(e.reshape(K_BLK // 8, 8, Q_BLK), axis=0)
                 total = t if total is None else total + t
                 o = dot(v_t[v_rows, rows], e.astype(BF16))
                 acc = o if acc is None else acc + o
             if unit_q is not None:
-                keys = jnp.concatenate([k_dup[head_q, rows, :], k_n[head_q // 2, rows, :]], axis=1)
-                s = dot(keys, q)
+                s = dot(k_n[head_q // 2, rows, :], q)
                 s_q[rows, :] = s
                 m = jnp.max(s.reshape(K_BLK // 8, 8, Q_BLK), axis=0)
                 new_max = m if new_max is None else jnp.maximum(new_max, m)
@@ -372,7 +362,7 @@
 
 
 def decoder_kernel(z_ref, rank_ref, pos_me, pos_x, qkv_hbm, proj_hbm, up_hbm, down_hbm, both_ref,
-                   qkv, proj, up, down, hid, norm, fin, q_3, k_n, k_dup, v_t, o_t, s_even, s_odd, w_sem, ready, row_send, row_recv, fin_send, fin_recv, pos, pos_sem):
+                   qkv, proj, up, down, hid, norm, fin, q_z, k_n, v_t, o_t, s_even, s_odd, w_sem, ready, row_send, row_recv, fin_send, fin_recv, pos, pos_sem):
     me = lax.axis_index('sp')
     chip = me // 2
     core = me - 2 * chip
@@ -415,17 +405,17 @@
     fill_rows(0, OWN, CHUNK, own_norm)
 
     def queries(layer):
-        fill_rows(0, OWN, WIDE, lambda rows: make_queries(rows, norm, qkv[layer, 0:DDIM], q_3))
+        fill_rows(0, OWN, WIDE, lambda rows: make_queries(rows, norm, qkv[layer, 0:DDIM], q_z))
 
     def keys(layer, start, count):
         fill_rows(start, count, WIDE, lambda rows: make_keys(
-            rows, norm, qkv[layer, DDIM:2 * DDIM], qkv[layer, 2 * DDIM:3 * DDIM], k_n, k_dup, v_t))
+            rows, norm, qkv[layer, DDIM:2 * DDIM], qkv[layer, 2 * DDIM:3 * DDIM], k_n, v_t))
 
     copies[0].wait()
     queries(0)
     keys(0, 0, SEQ)
     pl.semaphore_signal(ready, inc=1, device_id={'sp': sib}, device_id_type=MESH)
-    attention(0, OWN, q_3, k_n, k_dup, v_t, o_t, s_even, s_odd)
+    attention(0, OWN, q_z, k_n, v_t, o_t, s_even, s_odd)
     pl.semaphore_wait(ready, 1)
     for copy in copies[1:]:
         copy.wait()
@@ -458,7 +448,7 @@
         row_copy(i).wait()
     keys(1, OWN, OWN)
 
-    attention(0, TOK, q_3, k_n, k_dup, v_t, o_t, s_even, s_odd)
+    attention(0, TOK, q_z, k_n, v_t, o_t, s_even, s_odd)
     pieces = TOK // CHUNK
 
     def fin_copy(i):
@@ -483,7 +473,7 @@
 
     lax.fori_loop(0, pieces, functools.partial(last_mlp, start=0), 0)
     fin_copy(pieces - 1).start()
-    attention(TOK, TOK, q_3, k_n, k_dup, v_t, o_t, s_even, s_odd)
+    attention(TOK, TOK, q_z, k_n, v_t, o_t, s_even, s_odd)
     lax.fori_loop(0, pieces, functools.partial(last_mlp, start=TOK), 0)
     for i in range(pieces):
         fin_copy(i).wait()
@@ -503,9 +493,8 @@
             pltpu.VMEM((OWN, DDIM), BF16),
             pltpu.VMEM((SEQ, DDIM), BF16),
             pltpu.VMEM((TOK, DDIM), BF16),
-            pltpu.VMEM((DEC_HEADS, 4 * HEAD, OWN), BF16),
+            pltpu.VMEM((DEC_HEADS, PAIR, OWN), BF16),
             pltpu.VMEM((DEC_HEADS // 2, SEQ, PAIR), BF16),
-            pltpu.VMEM((DEC_HEADS, SEQ, PAIR), BF16),
             pltpu.VMEM((DDIM, SEQ), BF16),
             pltpu.VMEM((DDIM, OWN), BF16),
             pltpu.VMEM((SEQ, Q_BLK), F32),

time: 147 us -> 147 us (level)
  no operation moved by 1% of the time
where the time goes in v5:
time: 147 us
  Pallas kernels  147 us (100%)
    pallas_call x1, Pallas kernels, decode(): pl.pallas_call(decoder_kernel, out_shape=jax.ShapeDtypeStruct((CLIPS, TOK...  105 us
    pallas_call x1, Pallas kernels, encode(): pl.pallas_call(encoder_kernel, out_shape=(jax.ShapeDtypeStruct((ROWS + 2...  35.9 us
    pallas_call x1, Pallas kernels, project(): pl.pallas_call(output_kernel, out_shape=jax.ShapeDtypeStruct((CLIPS, TOK,...  6.25 us

profile of v5, /device:TPU:0, one launch (start us, length us, event | category | flops | bytes accessed | tf_op | source)
XLA Modules:
  0.0 147.1 jit_solution(2961140117914059303)
XLA Ops:
  0.0 35.9 %encoder.1 = (bf16[512,384]{1,0:T(8,128)(2,1)}, s32[8,768]{1,0:T(8,128)}, bf16[3,768,384]{2,1,0:T(8,128)(2,1)}) custom-call(s32[2,768]{1,0:T(2,128)} %mask_ref.1, bf16[768]{0:T(1024)(128)(2,1)} %bpe_ref.1, bf16[384]{0:T(512)(128)(2,1)} %token_ref.1, bf16[2,768,1536]{2,1,0:T(8,128)(2,1)} %patch_hbm.1, bf16[768,768]{1,0:T(8,128)(2,1)} %pos_hbm.1, ...), custom_call_target="tpu_custom_call" | custom-call | flops 12000000000 | bytes 40000000 | tf_op jit(solution)/shard_map/encoder/pallas_call | solution.py:236
  35.9 104.7 %decoder.1.both_ref = bf16[2,768,384]{2,1,0:T(8,128)(2,1)} custom-call(bf16[512,384]{1,0:T(8,128)(2,1)} %get-tuple-element.8.z_ref, s32[8,768]{1,0:T(8,128)} %get-tuple-element.9.rank_ref, bf16[768,384]{1,0:T(8,128)(2,1)} %pos_me.1, bf16[3,768,384]{2,1,0:T(8,128)(2,1)} %get-tuple-element.10.pos_x, bf16[2,1152,384]{2,1,0:T(8,128)(2,1)} %bitcast.10, ...), custom_call_target="tpu_custom_call" | custom-call | flops 60000002048 | bytes 20000000 | tf_op jit(solution)/shard_map/decoder/pallas_call | solution.py:483
  140.6 6.3 %output.1 = f32[2,768,1536]{2,1,0:T(8,128)} custom-call(bf16[2,768,384]{2,1,0:T(8,128)(2,1)} %decoder.1.both_ref, bf16[384,1536]{1,0:T(8,128)(2,1)} %w_ref.1), custom_call_target="tpu_custom_call" | custom-call | flops 2000000000 | bytes 12000000 | tf_op jit(solution)/shard_map/output/pallas_call | solution.py:538

commit v6 on v4

--- a/solution.py
+++ b/solution.py
@@ -278,7 +278,7 @@
     )(mask, bpe, token, patches, enc_pos, wpe, dec_pos, wed, qkv_t, proj, up, down)
 
 
-Q_BLK = 256
+Q_BLK = 512
 K_BLK = 256
 CHUNK = 256
 WIDE = 512
@@ -336,15 +336,22 @@
             head_p, cols_p = place(unit_p)
             shift = col_max(max8)
             v_rows = pl.ds(pl.multiple_of(head_p * HEAD, HEAD), HEAD)
-        new_max = total = acc = None
+        new_max = total = late = None
+        accs = [None, None]
+
+        def weigh(idx, weights):
+            o = dot(v_t[v_rows, idx * K_BLK:(idx + 1) * K_BLK], weights)
+            accs[idx % 2] = o if accs[idx % 2] is None else accs[idx % 2] + o
+
         for idx in range(SEQ // K_BLK):
             rows = slice(idx * K_BLK, (idx + 1) * K_BLK)
             if unit_p is not None:
                 e = jnp.exp2(s_p[rows, :] - shift)
                 t = jnp.sum(e.reshape(K_BLK // 8, 8, Q_BLK), axis=0)
                 total = t if total is None else total + t
-                o = dot(v_t[v_rows, rows], e.astype(BF16))
-                acc = o if acc is None else acc + o
+                if late is not None:
+                    weigh(*late)
+                late = (idx, e.astype(BF16))
             if unit_q is not None:
                 keys = jnp.concatenate([k_dup[head_q, rows, :], k_n[head_q // 2, rows, :]], axis=1)
                 s = dot(keys, q)
@@ -352,7 +359,8 @@
                 m = jnp.max(s.reshape(K_BLK // 8, 8, Q_BLK), axis=0)
                 new_max = m if new_max is None else jnp.maximum(new_max, m)
         if unit_p is not None:
-            o_t[v_rows, cols_p] = (acc * (1.0 / col_sum(total))).astype(BF16)
+            weigh(*late)
+            o_t[v_rows, cols_p] = ((accs[0] + accs[1]) * (1.0 / col_sum(total))).astype(BF16)
         return new_max
 
     first = mixed(0, s_even, None, None, None)
@@ -458,7 +466,8 @@
         row_copy(i).wait()
     keys(1, OWN, OWN)
 
-    attention(0, TOK, q_3, k_n, k_dup, v_t, o_t, s_even, s_odd)
+    early = 2 * Q_BLK
+    attention(0, early, q_3, k_n, k_dup, v_t, o_t, s_even, s_odd)
     pieces = TOK // CHUNK
 
     def fin_copy(i):
@@ -483,7 +492,7 @@
 
     lax.fori_loop(0, pieces, functools.partial(last_mlp, start=0), 0)
     fin_copy(pieces - 1).start()
-    attention(TOK, TOK, q_3, k_n, k_dup, v_t, o_t, s_even, s_odd)
+    attention(early, OWN - early, q_3, k_n, k_dup, v_t, o_t, s_even, s_odd)
     lax.fori_loop(0, pieces, functools.partial(last_mlp, start=TOK), 0)
     for i in range(pieces):
         fin_copy(i).wait()

time: 147 us -> 144 us (0.980)
  Pallas kernels: 147 us -> 144 us
    pallas_call x1, Pallas kernels: 105 us -> 102 us  [decode(): pl.pallas_call(decoder_kernel, out_shape=jax.ShapeDtypeStruct((CLIPS, TOK...]
where the time goes in v6:
time: 144 us
  Pallas kernels  144 us (100%)
    pallas_call x1, Pallas kernels, decode(): pl.pallas_call(decoder_kernel, out_shape=jax.ShapeDtypeStruct((CLIPS, TOK...  102 us
    pallas_call x1, Pallas kernels, encode(): pl.pallas_call(encoder_kernel, out_shape=(jax.ShapeDtypeStruct((ROWS + 2...  35.9 us
    pallas_call x1, Pallas kernels, project(): pl.pallas_call(output_kernel, out_shape=jax.ShapeDtypeStruct((CLIPS, TOK,...  6.26 us

profile of v6, /device:TPU:0, one launch (start us, length us, event | category | flops | bytes accessed | tf_op | source)
XLA Modules:
  0.0 143.9 jit_solution(8491000207687621432)
XLA Ops:
  0.0 35.9 %encoder.1 = (bf16[512,384]{1,0:T(8,128)(2,1)}, s32[8,768]{1,0:T(8,128)}, bf16[3,768,384]{2,1,0:T(8,128)(2,1)}) custom-call(s32[2,768]{1,0:T(2,128)} %mask_ref.1, bf16[768]{0:T(1024)(128)(2,1)} %bpe_ref.1, bf16[384]{0:T(512)(128)(2,1)} %token_ref.1, bf16[2,768,1536]{2,1,0:T(8,128)(2,1)} %patch_hbm.1, bf16[768,768]{1,0:T(8,128)(2,1)} %pos_hbm.1, ...), custom_call_target="tpu_custom_call" | custom-call | flops 12000000000 | bytes 40000000 | tf_op jit(solution)/shard_map/encoder/pallas_call | solution.py:236
  35.9 101.5 %decoder.1.both_ref = bf16[2,768,384]{2,1,0:T(8,128)(2,1)} custom-call(bf16[512,384]{1,0:T(8,128)(2,1)} %get-tuple-element.8.z_ref, s32[8,768]{1,0:T(8,128)} %get-tuple-element.9.rank_ref, bf16[768,384]{1,0:T(8,128)(2,1)} %pos_me.1, bf16[3,768,384]{2,1,0:T(8,128)(2,1)} %get-tuple-element.10.pos_x, bf16[2,1152,384]{2,1,0:T(8,128)(2,1)} %bitcast.10, ...), custom_call_target="tpu_custom_call" | custom-call | flops 60000002048 | bytes 20000000 | tf_op jit(solution)/shard_map/decoder/pallas_call | solution.py:502
  137.4 6.3 %output.1 = f32[2,768,1536]{2,1,0:T(8,128)} custom-call(bf16[2,768,384]{2,1,0:T(8,128)(2,1)} %decoder.1.both_ref, bf16[384,1536]{1,0:T(8,128)(2,1)} %w_ref.1), custom_call_target="tpu_custom_call" | custom-call | flops 2000000000 | bytes 12000000 | tf_op jit(solution)/shard_map/output/pallas_call | solution.py:558

commit v7 on v6

--- a/solution.py
+++ b/solution.py
@@ -114,8 +114,8 @@
 
     bias = bpe_ref[...].astype(F32).reshape(1, DIM)
 
-    def window(clip, slots):
-        rows = lax.broadcasted_iota(jnp.int32, (WIN, TOK), 0).astype(F32)
+    def window(clip, slots, low, count):
+        rows = (lax.broadcasted_iota(jnp.int32, (count, TOK), 0) + low).astype(F32)
         hit = jnp.where(rows == slots, 1.0, 0.0)
         select = hit.astype(BF16)
         moved = dot(select, patch[clip]).astype(BF16)
@@ -125,11 +125,14 @@
 
     far = jnp.where(chip == 0, slot_of[1:2], slot_of[0:1])
     near = jnp.where(chip == 0, slot_of[0:1], slot_of[1:2])
-    sendbuf[...] = window(1 - chip, far)
-    to_peer = send(sendbuf, win.at[1], win_send.at[0], win_recv.at[0], peer)
+    halves = [pl.ds(0, VIS), pl.ds(VIS, VIS)]
+    to_peer = []
+    for idx, part in enumerate(halves):
+        sendbuf[idx * VIS:(idx + 1) * VIS] = window(1 - chip, far, idx * VIS, VIS)
+        to_peer.append(send(sendbuf.at[part], win.at[1, part], win_send.at[idx], win_recv.at[idx], peer))
     near_load.wait()
-    win[0] = window(chip, near)
-    to_sib = send(win.at[0], win.at[2], win_send.at[1], win_recv.at[1], sib)
+    win[0] = window(chip, near, 0, WIN)
+    to_sib = send(win.at[0], win.at[2], win_send.at[2], win_recv.at[2], sib)
 
     for copy in mask_copies:
         copy.wait()
@@ -157,14 +160,17 @@
     even = core == 0
     left, right = placement(1), placement(3)
     place = [placement(0), placement(2), jnp.where(even, right, left), jnp.where(even, left, right)]
-    to_peer.wait_recv()
-    relay = send(win.at[1], win.at[3], win_send.at[2], win_recv.at[2], sib)
+    relay = []
+    for idx, part in enumerate(halves):
+        to_peer[idx].wait_recv()
+        relay.append(send(win.at[1, part], win.at[3, part], win_send.at[3 + idx], win_recv.at[3 + idx], sib))
     pos_peer = send(dec_pos_hbm, pos_out.at[0], pos_send.at[0], pos_recv.at[0], peer)
     pos_sib = send(dec_pos_hbm, pos_out.at[1], pos_send.at[1], pos_recv.at[1], sib)
     total = dot(place[0].astype(BF16), win[0]) + dot(place[1].astype(BF16), win[1])
     to_sib.wait_recv()
     total = total + dot(place[2].astype(BF16), win[2])
-    relay.wait_recv()
+    for copy in relay:
+        copy.wait_recv()
     total = total + dot(place[3].astype(BF16), win[3])
     hall[...] = total.astype(BF16)
     own = pl.ds(pl.multiple_of(core * MINE, MINE), MINE)
@@ -223,9 +229,8 @@
     first = lax.broadcasted_iota(jnp.int32, (2 * HEAD, DDIM), 0) == 0
     z_ref[ROWS:] = jnp.where(first, token_ref[...].astype(F32).reshape(1, DDIM), 0.0).astype(BF16)
     last = send(z_ref.at[own], z_ref.at[own], row_send.at[LAYERS - 1], row_recv.at[LAYERS - 1], sib)
-    to_peer.wait_send()
-    to_sib.wait_send()
-    relay.wait_send()
+    for copy in (*to_peer, to_sib, *relay):
+        copy.wait_send()
     pos_peer.wait_send()
     pos_sib.wait()
     pos_diag.wait()
@@ -265,8 +270,8 @@
             pltpu.SemaphoreType.DMA((LAYERS * 4,)),
             pltpu.SemaphoreType.DMA((SP - 1,)),
             pltpu.SemaphoreType.DMA((SP - 1,)),
-            pltpu.SemaphoreType.DMA((3,)),
-            pltpu.SemaphoreType.DMA((3,)),
+            pltpu.SemaphoreType.DMA((5,)),
+            pltpu.SemaphoreType.DMA((5,)),
             pltpu.SemaphoreType.DMA((3,)),
             pltpu.SemaphoreType.DMA((3,)),
             pltpu.SemaphoreType.DMA((LAYERS,)),
@@ -320,13 +325,18 @@
     v_t[:, rows] = dot_nt(w_v, a).astype(BF16)
 
 
-def attention(start, count, q_3, k_n, k_dup, v_t, o_t, s_even, s_odd):
+def attention(start, count, q_3, k_n, k_dup, v_t, o_t, s_even, s_odd, first=None, follow=None):
     blocks = count // Q_BLK
     units = DEC_HEADS * blocks
 
     def place(unit):
         head = unit // blocks
-        return head, pl.ds(pl.multiple_of(start + (unit - head * blocks) * Q_BLK, Q_BLK), Q_BLK)
+        offset = start + (unit - head * blocks) * Q_BLK
+        if follow is not None:
+            past = unit >= units
+            head = jnp.where(past, 0, head)
+            offset = jnp.where(past, follow, offset)
+        return head, pl.ds(pl.multiple_of(offset, Q_BLK), Q_BLK)
 
     def mixed(unit_q, s_q, unit_p, s_p, max8):
         if unit_q is not None:
@@ -363,14 +373,16 @@
             o_t[v_rows, cols_p] = ((accs[0] + accs[1]) * (1.0 / col_sum(total))).astype(BF16)
         return new_max
 
-    first = mixed(0, s_even, None, None, None)
+    if first is None:
+        first = mixed(0, s_even, None, None, None)
 
     def body(i, max8):
         unit = 2 * i
         max_odd = mixed(unit + 1, s_odd, unit, s_even, max8)
-        return mixed(jnp.minimum(unit + 2, units - 1), s_even, unit + 1, s_odd, max_odd)
-
-    lax.fori_loop(0, units // 2, body, first)
+        following = unit + 2 if follow is not None else jnp.minimum(unit + 2, units - 1)
+        return mixed(following, s_even, unit + 1, s_odd, max_odd)
+
+    return lax.fori_loop(0, units // 2, body, first)
 
 
 def mlp(rows, hid, o_t, w_proj, w_up, w_down):
@@ -467,7 +479,7 @@
     keys(1, OWN, OWN)
 
     early = 2 * Q_BLK
-    attention(0, early, q_3, k_n, k_dup, v_t, o_t, s_even, s_odd)
+    scored = attention(0, early, q_3, k_n, k_dup, v_t, o_t, s_even, s_odd, follow=early)
     pieces = TOK // CHUNK
 
     def fin_copy(i):
@@ -492,7 +504,7 @@
 
     lax.fori_loop(0, pieces, functools.partial(last_mlp, start=0), 0)
     fin_copy(pieces - 1).start()
-    attention(early, OWN - early, q_3, k_n, k_dup, v_t, o_t, s_even, s_odd)
+    attention(early, OWN - early, q_3, k_n, k_dup, v_t, o_t, s_even, s_odd, first=scored)
     lax.fori_loop(0, pieces, functools.partial(last_mlp, start=TOK), 0)
     for i in range(pieces):
         fin_copy(i).wait()

time: 144 us -> 143 us (level)
  no operation moved by 1% of the time
where the time goes in v7:
time: 143 us
  Pallas kernels  143 us (100%)
    pallas_call x1, Pallas kernels, decode(): pl.pallas_call(decoder_kernel, out_shape=jax.ShapeDtypeStruct((CLIPS, TOK...  101 us
    pallas_call x1, Pallas kernels, encode(): pl.pallas_call(encoder_kernel, out_shape=(jax.ShapeDtypeStruct((ROWS + 2...  35.8 us
    pallas_call x1, Pallas kernels, project(): pl.pallas_call(output_kernel, out_shape=jax.ShapeDtypeStruct((CLIPS, TOK,...  6.26 us

profile of v7, /device:TPU:0, one launch (start us, length us, event | category | flops | bytes accessed | tf_op | source)
XLA Modules:
  0.0 142.8 jit_solution(9173982341282677832)
XLA Ops:
  0.0 35.8 %encoder.1 = (bf16[512,384]{1,0:T(8,128)(2,1)}, s32[8,768]{1,0:T(8,128)}, bf16[3,768,384]{2,1,0:T(8,128)(2,1)}) custom-call(s32[2,768]{1,0:T(2,128)} %mask_ref.1, bf16[768]{0:T(1024)(128)(2,1)} %bpe_ref.1, bf16[384]{0:T(512)(128)(2,1)} %token_ref.1, bf16[2,768,1536]{2,1,0:T(8,128)(2,1)} %patch_hbm.1, bf16[768,768]{1,0:T(8,128)(2,1)} %pos_hbm.1, ...), custom_call_target="tpu_custom_call" | custom-call | flops 12000000000 | bytes 40000000 | tf_op jit(solution)/shard_map/encoder/pallas_call | solution.py:241
  35.8 100.6 %decoder.1.both_ref = bf16[2,768,384]{2,1,0:T(8,128)(2,1)} custom-call(bf16[512,384]{1,0:T(8,128)(2,1)} %get-tuple-element.8.z_ref, s32[8,768]{1,0:T(8,128)} %get-tuple-element.9.rank_ref, bf16[768,384]{1,0:T(8,128)(2,1)} %pos_me.1, bf16[3,768,384]{2,1,0:T(8,128)(2,1)} %get-tuple-element.10.pos_x, bf16[2,1152,384]{2,1,0:T(8,128)(2,1)} %bitcast.10, ...), custom_call_target="tpu_custom_call" | custom-call | flops 60000002048 | bytes 20000000 | tf_op jit(solution)/shard_map/decoder/pallas_call | solution.py:514
  136.3 6.3 %output.1 = f32[2,768,1536]{2,1,0:T(8,128)} custom-call(bf16[2,768,384]{2,1,0:T(8,128)(2,1)} %decoder.1.both_ref, bf16[384,1536]{1,0:T(8,128)(2,1)} %w_ref.1), custom_call_target="tpu_custom_call" | custom-call | flops 2000000000 | bytes 12000000 | tf_op jit(solution)/shard_map/output/pallas_call | solution.py:570

commit v8 on v7

--- a/solution.py
+++ b/solution.py
@@ -540,13 +540,13 @@
             pltpu.VMEM((SP, TOK, DDIM), BF16),
             pltpu.SemaphoreType.DMA((SP,)),
         ],
-        compiler_params=pltpu.CompilerParams(collective_id=1, has_side_effects=True, vmem_limit_bytes=58 * 2 ** 20),
+        compiler_params=pltpu.CompilerParams(collective_id=1, has_side_effects=True, vmem_limit_bytes=54 * 2 ** 20),
         cost_estimate=pl.CostEstimate(flops=60 * 10 ** 9, bytes_accessed=2 * 10 ** 7, transcendentals=6 * 10 ** 7),
         name='decoder',
     )(z, rank, pos, pos_x, wqkv, wproj, wup, wdown)
 
 
-def output_kernel(both_ref, w_ref, out_hbm, buf, sem):
+def output_kernel(both_hbm, w_ref, out_hbm, both, buf, in_sem, sem):
     pieces = TOK // CHUNK
 
     def out_copy(i):
@@ -554,10 +554,17 @@
         rows = pl.ds(pl.multiple_of((i - clip * pieces) * CHUNK, CHUNK), CHUNK)
         return pltpu.make_async_copy(buf.at[i], out_hbm.at[clip, rows], sem.at[i])
 
-    def body(i, carry):
+    def in_copy(i):
         clip = i // pieces
         rows = pl.ds(pl.multiple_of((i - clip * pieces) * CHUNK, CHUNK), CHUNK)
-        buf[i] = dot(both_ref[clip, rows, :], w_ref[...])
+        return pltpu.make_async_copy(both_hbm.at[clip, rows], both.at[i], in_sem.at[i])
+
+    for i in range(CLIPS * pieces):
+        in_copy(i).start()
+
+    def body(i, carry):
+        in_copy(i).wait()
+        buf[i] = dot(both[i], w_ref[...])
         out_copy(i).start()
         return carry
 
@@ -570,13 +577,15 @@
     return pl.pallas_call(
         output_kernel,
         out_shape=jax.ShapeDtypeStruct((CLIPS, TOK, PATCH), F32),
-        in_specs=[VMEM] * 2,
+        in_specs=[pl.BlockSpec(memory_space=pltpu.HBM), VMEM],
         out_specs=ANY,
         scratch_shapes=[
+            pltpu.VMEM((CLIPS * TOK // CHUNK, CHUNK, DDIM), BF16),
             pltpu.VMEM((CLIPS * TOK // CHUNK, CHUNK, PATCH), F32),
             pltpu.SemaphoreType.DMA((CLIPS * TOK // CHUNK,)),
+            pltpu.SemaphoreType.DMA((CLIPS * TOK // CHUNK,)),
         ],
-        compiler_params=pltpu.CompilerParams(vmem_limit_bytes=62 * 2 ** 20),
+        compiler_params=pltpu.CompilerParams(vmem_limit_bytes=20 * 2 ** 20),
         cost_estimate=pl.CostEstimate(flops=2 * 10 ** 9, bytes_accessed=12 * 10 ** 6, transcendentals=0),
         name='output',
     )(both, w_out)

time: 143 us -> 144 us (level)
  no operation moved by 1% of the time
where the time goes in v8:
time: 144 us
  Pallas kernels  143 us (99%)
    pallas_call x1, Pallas kernels, decode(): pl.pallas_call(decoder_kernel, out_shape=jax.ShapeDtypeStruct((CLIPS, TOK...  101 us
    pallas_call x1, Pallas kernels, encode(): pl.pallas_call(encoder_kernel, out_shape=(jax.ShapeDtypeStruct((ROWS + 2...  35.8 us
    pallas_call x1, Pallas kernels, project(): pl.pallas_call(output_kernel, out_shape=jax.ShapeDtypeStruct((CLIPS, TOK,...  6.18 us

profile of v8, /device:TPU:0, one launch (start us, length us, event | category | flops | bytes accessed | tf_op | source)
XLA Modules:
  0.0 144.1 jit_solution(2705447422926177382)
XLA Ops:
  0.0 35.8 %encoder.1 = (bf16[512,384]{1,0:T(8,128)(2,1)}, s32[8,768]{1,0:T(8,128)}, bf16[3,768,384]{2,1,0:T(8,128)(2,1)}) custom-call(s32[2,768]{1,0:T(2,128)} %mask_ref.1, bf16[768]{0:T(1024)(128)(2,1)} %bpe_ref.1, bf16[384]{0:T(512)(128)(2,1)} %token_ref.1, bf16[2,768,1536]{2,1,0:T(8,128)(2,1)} %patch_hbm.1, bf16[768,768]{1,0:T(8,128)(2,1)} %pos_hbm.1, ...), custom_call_target="tpu_custom_call" | custom-call | flops 12000000000 | bytes 40000000 | tf_op jit(solution)/shard_map/encoder/pallas_call | solution.py:241
  35.8 0.0 copy-start
  35.8 100.7 %decoder.1.both_hbm = bf16[2,768,384]{2,1,0:T(8,128)(2,1)} custom-call(bf16[512,384]{1,0:T(8,128)(2,1)} %get-tuple-element.8.z_ref, s32[8,768]{1,0:T(8,128)} %get-tuple-element.9.rank_ref, bf16[768,384]{1,0:T(8,128)(2,1)} %pos_me.1, bf16[3,768,384]{2,1,0:T(8,128)(2,1)} %get-tuple-element.10.pos_x, bf16[2,1152,384]{2,1,0:T(8,128)(2,1)} %bitcast.10, ...), custom_call_target="tpu_custom_call" | custom-call | flops 60000002048 | bytes 20000000 | tf_op jit(solution)/shard_map/decoder/pallas_call | solution.py:514
  136.5 0.0 copy-done
  136.5 0.0 copy-start.1
  136.5 1.3 copy-done.1
  137.7 6.2 %output.1 = f32[2,768,1536]{2,1,0:T(8,128)} custom-call(bf16[2,768,384]{2,1,0:T(8,128)(2,1)S(1)} %copy-done.1, bf16[384,1536]{1,0:T(8,128)(2,1)S(1)} %copy-done), custom_call_target="tpu_custom_call" | custom-call | flops 2000000000 | bytes 12000000 | tf_op jit(solution)/shard_map/output/pallas_call | solution.py:577
Async XLA Ops:
  35.8 100.7 %copy-start = (bf16[384,1536]{1,0:T(8,128)(2,1)S(1)}, bf16[384,1536]{1,0:T(8,128)(2,1)}, u32[]{:S(2)}) copy-start(bf16[384,1536]{1,0:T(8,128)(2,1)} %w_ref.1) | copy-start | bytes 3538948
  136.5 1.3 copy-start.1
